TPU v7x, 256 devices: a whole 4x4x8 slice. The times are simulated.
256 devices in a mesh: trunk: 8 (over x, core), branch: 32 (over z, y).
Axes of the slice: x: 4, y: 4, z: 8, core: 2. Of those that a mesh axis runs over, the one named last changes fastest.
Arguments:
- queries: bfloat16 [8, 4096, 4096], P('trunk', 'branch'), may hold values from -160 to 160
- keys_values: bfloat16 [8, 4096, 2, 512], P('trunk', 'branch'), may hold values from -7 to 7
- out_grad: bfloat16 [8, 4096, 4096], P('trunk', 'branch'), may hold values from -6 to 6
- trunk_kv: bfloat16 [8, 32, 2, 16, 512], P('trunk', 'branch'), may hold values from -6 to 6
- branch_of: int32 [8, 4096], P('trunk', 'branch'), may hold values from 0 to 63, never falling along the last dimension, each value on 1 to 128 neighbouring positions
- branch_reach: int32 [8, 64], P('trunk'), may hold values from 1 to 8
- ancestors: int32 [8, 32, 8], P('trunk', 'branch'), may hold values from 0 to 31
Outputs:
- attended: bfloat16 [8, 4096, 4096], P('trunk', 'branch')
- query_grad: bfloat16 [8, 4096, 4096], P('trunk', 'branch')
- kv_grad: float32 [8, 4096, 2, 512], P('trunk', 'branch')
- trunk_grad: float32 [8, 32, 2, 16, 512], P('trunk', 'branch')
Inputs may be any that keep to these rules, and one draw needn't show every extreme that they name: `branch_of`: ids never fall along a row; each branch covers 1 to 128 consecutive tokens. `ancestors`: entry d names the branch index of the device at trunk index d that holds the segment read at depth d.
All inputs are finite; a program needn't handle non-finite values.
Results may differ from a plain program's by a relative error of at most 0.005.
Values may be sent and summed in bfloat16 or wider, within the bound.
A program may use at most 128 MiB of HBM per device.

v0:
```python
import math

import jax
import jax.numpy as jnp
from jax import lax
from jax.sharding import PartitionSpec as P

HQ = 32
KVH = 4
DH = 128


def laid_out(pieces, dim):
    dims = list(pieces.shape[1:])
    dims[dim] *= pieces.shape[0]
    return jnp.moveaxis(pieces, 0, dim).reshape(dims)


def sent_to_all(array, axis):
    size = lax.axis_size(axis)
    return lax.all_to_all(
        jnp.broadcast_to(array[None], (size, *array.shape)), axis, 0, 0, tiled=True
    )


def gather_directly(array, axis, dim):
    return laid_out(sent_to_all(array, axis), dim)


def from_behind(block, axis, distance):
    devices = range(lax.axis_size(axis))
    route = [(i - distance, i) for i in devices if i - distance in devices]
    return lax.ppermute(block, axis, route)


def split_up(array, dim, size):
    before, after = (array.shape[:dim], array.shape[dim + 1 :])
    return jnp.moveaxis(array.reshape(*before, size, -1, *after), dim, 0)


def summed_on_arrival(array, axis, dim):
    pieces = split_up(array, dim, lax.axis_size(axis))
    arrived = lax.all_to_all(pieces, axis, split_axis=0, concat_axis=0, tiled=True)
    return arrived.astype(jnp.float32).sum(axis=0)


def build_allowed(tags, earlier_tags, reach_rows, seg_len, depth_count):
    trunk_depth = jnp.arange(depth_count * seg_len, dtype=jnp.int32) // seg_len
    trunk_ok = trunk_depth[None, :] < reach_rows[:, None]
    earlier_ok = earlier_tags[None, :] == tags[:, None]
    position = jnp.arange(tags.shape[0], dtype=jnp.int32)
    own_ok = (tags[None, :] == tags[:, None]) & (position[None, :] <= position[:, None])
    return jnp.concatenate([trunk_ok, earlier_ok, own_ok], axis=1)


def attend_block(query_rows, grad_rows, key_rows, value_rows, allowed):
    head_scale = 1.0 / math.sqrt(DH)
    group = HQ // KVH
    n_rows = query_rows.shape[0]
    outputs, query_grads, key_grads, value_grads = ([], [], [], [])
    for head_group in range(KVH):
        query_part = query_rows[:, head_group * group * DH : (head_group + 1) * group * DH].reshape(
            n_rows, group, DH
        )
        grad_part = grad_rows[:, head_group * group * DH : (head_group + 1) * group * DH].reshape(
            n_rows, group, DH
        )
        key_part = key_rows[:, head_group * DH : (head_group + 1) * DH]
        value_part = value_rows[:, head_group * DH : (head_group + 1) * DH]
        scores = (
            jnp.einsum("qrd,kd->rqk", query_part, key_part, preferred_element_type=jnp.float32)
            * head_scale
        )
        masked = jnp.where(allowed[None], scores, -1e30)
        highest = jnp.max(masked, axis=-1, keepdims=True)
        expo = jnp.exp(masked - highest)
        weights = expo / jnp.sum(expo, axis=-1, keepdims=True)
        weights_bf = weights.astype(jnp.bfloat16)
        output = jnp.einsum(
            "rqk,kd->qrd", weights_bf, value_part, preferred_element_type=jnp.float32
        ).reshape(n_rows, group * DH)
        grad_weights = jnp.einsum(
            "qrd,kd->rqk", grad_part, value_part, preferred_element_type=jnp.float32
        )
        row_mean = jnp.sum(weights * grad_weights, axis=-1, keepdims=True)
        score_grad = (weights * (grad_weights - row_mean)).astype(jnp.bfloat16)
        outputs.append(output)
        query_grads.append(
            (
                jnp.einsum("rqk,kd->qrd", score_grad, key_part, preferred_element_type=jnp.float32)
                * head_scale
            ).reshape(n_rows, group * DH)
        )
        key_grads.append(
            jnp.einsum("rqk,qrd->kd", score_grad, query_part, preferred_element_type=jnp.float32)
            * head_scale
        )
        value_grads.append(
            jnp.einsum("rqk,qrd->kd", weights_bf, grad_part, preferred_element_type=jnp.float32)
        )
    attended = jnp.concatenate(outputs, axis=1).astype(jnp.bfloat16)
    query_grad = jnp.concatenate(query_grads, axis=1).astype(jnp.bfloat16)
    return (
        attended,
        query_grad,
        jnp.concatenate(key_grads, axis=1),
        jnp.concatenate(value_grads, axis=1),
    )


def on_device(queries, keys_values, out_grad, trunk_kv, branch_of, branch_reach, ancestors):
    depth_count = lax.axis_size("trunk")
    n_branch = lax.axis_size("branch")
    seg_len = trunk_kv.shape[3]
    width = trunk_kv.shape[4]
    block_len = queries.shape[1]
    trunk_len = depth_count * seg_len
    requested = lax.all_to_all(ancestors[0, 0], "trunk", split_axis=0, concat_axis=0, tiled=True)
    own_segment = trunk_kv[0]
    piece = gather_directly(own_segment, "branch", 0)
    owner_index = jnp.arange(piece.shape[0], dtype=jnp.int32)
    hits = (requested[:, None] == owner_index[None, :]).astype(jnp.bfloat16)
    chosen = jnp.einsum("tn,nslc->tslc", hits, piece, preferred_element_type=jnp.float32)
    picked = chosen.astype(jnp.bfloat16)
    fetched = lax.all_to_all(picked, "trunk", split_axis=0, concat_axis=0, tiled=True)
    branch_ids = branch_of[0]
    tags = branch_ids + 1
    earlier_kv, earlier_tags = from_behind((keys_values[0], tags), "branch", 1)
    reach_table = branch_reach[0]
    branch_index = jnp.arange(reach_table.shape[0], dtype=jnp.int32)
    reach_rows = jnp.sum(
        jnp.where(branch_ids[:, None] == branch_index[None, :], reach_table[None, :], 0), axis=1
    )
    allowed = build_allowed(tags, earlier_tags, reach_rows, seg_len, depth_count)
    key_rows = jnp.concatenate(
        [fetched[:, 0].reshape(trunk_len, width), earlier_kv[:, 0], keys_values[0, :, 0]], axis=0
    )
    value_rows = jnp.concatenate(
        [fetched[:, 1].reshape(trunk_len, width), earlier_kv[:, 1], keys_values[0, :, 1]], axis=0
    )
    attended, query_grad, key_grad, value_grad = attend_block(
        queries[0], out_grad[0], key_rows, value_rows, allowed
    )
    earlier_part = jnp.stack(
        [
            key_grad[trunk_len : trunk_len + block_len],
            value_grad[trunk_len : trunk_len + block_len],
        ],
        axis=1,
    )
    own_part = jnp.stack(
        [key_grad[trunk_len + block_len :], value_grad[trunk_len + block_len :]], axis=1
    )
    from_next = from_behind(earlier_part.astype(jnp.bfloat16), "branch", -1).astype(
        earlier_part.dtype
    )
    kv_grad = (own_part + from_next)[None]
    trunk_part = jnp.stack(
        [
            key_grad[:trunk_len].reshape(depth_count, seg_len, width),
            value_grad[:trunk_len].reshape(depth_count, seg_len, width),
        ],
        axis=1,
    )
    returned = lax.all_to_all(
        trunk_part.astype(jnp.bfloat16), "trunk", split_axis=0, concat_axis=0, tiled=True
    ).astype(trunk_part.dtype)
    owner_index = jnp.arange(n_branch, dtype=jnp.int32)
    owners_hit = (requested[None, :] == owner_index[:, None]).astype(jnp.float32)
    mine = summed_on_arrival(
        jnp.einsum("ot,tslc->oslc", owners_hit, returned, precision=lax.Precision.HIGHEST).astype(
            jnp.bfloat16
        ),
        "branch",
        0,
    )
    trunk_grad = mine[None]
    return (attended[None], query_grad[None], kv_grad, trunk_grad)


def solution(mesh):
    return jax.shard_map(
        on_device,
        mesh=mesh,
        in_specs=(
            P("trunk", "branch", None),
            P("trunk", "branch", None, None),
            P("trunk", "branch", None),
            P("trunk", "branch", None, None, None),
            P("trunk", "branch"),
            P("trunk", None),
            P("trunk", "branch", None),
        ),
        out_specs=(
            P("trunk", "branch", None),
            P("trunk", "branch", None),
            P("trunk", "branch", None, None),
            P("trunk", "branch", None, None, None),
        ),
        check_vma=False,
    )
```

profile of v0, /device:TPU:24, one launch (start us, length us, event | category | flops | bytes accessed | tf_op | source)
XLA Modules:
  0.0 156.9 jit_solution(16119084204471931922)
XLA Ops:
  0.6 0.7 copy.221
  1.4 9.3 %all_to_all.29 = s32[8,1,1]{2,1,0:T(1,128)} all-to-all(s32[8,1,1]{2,1,0:T(1,128)S(1)} %copy.221), channel_id=1, replica_groups=mesh['trunk'=8,'branch'=32] {'trunk'}, dimensions={0} | all-to-all | bytes 64 | tf_op jit(solution)/shard_map/all_to_all | solution.py:118
  10.7 1.9 %broadcast_in_dim.47 = bf16[32,1,2,16,512]{4,3,2,1,0:T(8,128)(2,1)} broadcast(bf16[2,16,512]{2,1,0:T(8,128)(2,1)} %bitcast.386), dimensions={2,3,4} | broadcast | bytes 1081344 | tf_op jit(solution)/shard_map/broadcast_in_dim | solution.py:22
  12.6 11.6 %all-to-all-start.1 = ((bf16[32,1,2,16,512]{4,3,2,1,0:T(8,128)(2,1)}), bf16[32,1,2,16,512]{4,3,2,1,0:T(8,128)(2,1)S(1)}, u32[]{:S(2)}, u32[]{:S(2)}) async-start(bf16[32,1,2,16,512]{4,3,2,1,0:T(8,128)(2,1)} %broadcast_in_dim.47), calls=%async_computation.1 | async-start | bytes 2097152 | tf_op jit(solution)/shard_map/all_to_all | solution.py:21
  24.2 0.5 broadcast_add_fusion
  24.7 3.4 %collective-permute-start.1 = (s32[128]{0:T(128)}, s32[128]{0:T(128)}, u32[]{:S(2)}, u32[]{:S(2)}) collective-permute-start(s32[128]{0:T(128)} %broadcast_add_fusion), channel_id=1, source_target_pairs={{0,1},{1,2},{2,3},{3,4},{4,5},{5,6},{6,7},{7,8},{8,9},{9,10},{10,1... | collective-permute-start | bytes 1544 | tf_op jit(solution)/shard_map/ppermute | solution.py:33
  28.1 3.4 %collective-permute-start = (bf16[128,2,512]{2,0,1:T(8,128)(2,1)S(1)}, bf16[128,2,512]{2,0,1:T(8,128)(2,1)}, u32[]{:S(2)}, u32[]{:S(2)}) collective-permute-start(bf16[128,2,512]{2,0,1:T(8,128)(2,1)S(1)} %bitcast.348), channel_id=1, source_target_pairs={{0,1},{1,2},{2,3},{3,4},{4,5},{5,6},{6,7},{7,8},{8,9},{9,10},{10,1... | collective-permute-start | bytes 786440 | tf_op jit(solution)/shard_map/ppermute | solution.py:33
  31.5 0.7 copy.229
  32.2 1.6 %copy.246 = bf16[1,128,4096]{1,2,0:T(8,128)(2,1)S(1)} copy(bf16[1,128,4096]{2,1,0:T(8,128)(2,1)} %param.9) | data formatting | bytes 2097152 | tf_op args[2]
  34.1 0.7 slice_bitcast_fusion.4
  34.7 1.0 fusion.71
  35.7 0.9 fusion.70
  36.9 10.5 %collective-permute-done.1 = s32[128]{0:T(128)} collective-permute-done((s32[128]{0:T(128)}, s32[128]{0:T(128)}, u32[]{:S(2)}, u32[]{:S(2)}) %collective-permute-start.1) | collective-permute-done | bytes 544 | tf_op jit(solution)/shard_map/ppermute | solution.py:33
  47.4 0.8 broadcast_compare_fusion
  48.2 0.6 pad_add_fusion
  48.8 4.2 %all-to-all-done.1 = bf16[32,1,2,16,512]{4,3,2,1,0:T(8,128)(2,1)S(1)} async-done(((bf16[32,1,2,16,512]{4,3,2,1,0:T(8,128)(2,1)}), bf16[32,1,2,16,512]{4,3,2,1,0:T(8,128)(2,1)S(1)}, u32[]{:S(2)}, u32[]{:S(2)}) %all-to-all-start.1) | async-done | bytes 1048608 | tf_op jit(solution)/shard_map/all_to_all | solution.py:21
  53.0 0.7 convolution_convert_fusion.1
  53.7 0.8 copy.223
  54.5 3.7 %all-to-all-start.2 = ((bf16[8,2,16,512]{3,2,1,0:T(8,128)(2,1)}), bf16[8,2,16,512]{3,2,1,0:T(8,128)(2,1)S(1)}, u32[]{:S(2)}, u32[]{:S(2)}) async-start(bf16[8,2,16,512]{3,2,1,0:T(8,128)(2,1)} %copy.223), calls=%async_computation.2 | async-start | bytes 524288 | tf_op jit(solution)/shard_map/all_to_all | solution.py:125
  58.2 1.0 slice_bitcast_fusion.5
  59.2 6.2 %all-to-all-done.2 = bf16[8,2,16,512]{3,2,1,0:T(8,128)(2,1)S(1)} async-done(((bf16[8,2,16,512]{3,2,1,0:T(8,128)(2,1)}), bf16[8,2,16,512]{3,2,1,0:T(8,128)(2,1)S(1)}, u32[]{:S(2)}, u32[]{:S(2)}) %all-to-all-start.2) | async-done | bytes 262176 | tf_op jit(solution)/shard_map/all_to_all | solution.py:125
  65.6 0.6 fusion.75
  66.2 0.9 convolution_bitcast_fusion
  67.1 1.6 %convolution_convert_fusion.2 = bf16[128,8,128]{2,0,1:T(8,128)(2,1)} fusion(bf16[384,512]{1,0:T(8,128)(2,1)S(1)} %get-tuple-element.62, f32[8,128]{1,0:T(8,128)S(1)} %get-tuple-element.46, bf16[128,8,128]{0,2,1:T(8,128)(2,1)S(1)} %bitcast.367, pred[128,384]{0,1:T(8,128)(4,1)S(1)} %copy-done.29, bf16[384,512]{1,0:T(8,128)(2,1)S(1)} %get-tuple-element.63), kind=kOutput, calls=%fused_computation.48 | convolution fusion | flops 203425152 | bytes 774144 | tf_op jit(solution)/shard_map/rqk,kd->qrd/dot_general | solution.py:79
  69.4 0.4 fusion.29
  70.3 0.6 fusion.76
  71.0 2.5 %convolution_convert_fusion.3 = bf16[128,8,128]{2,0,1:T(8,128)(2,1)} fusion(bf16[384,512]{1,0:T(8,128)(2,1)} %copy-done.22, f32[8,128]{1,0:T(8,128)S(1)} %get-tuple-element.48, bf16[128,8,128]{0,2,1:T(8,128)(2,1)S(1)} %bitcast.362, pred[128,384]{0,1:T(8,128)(4,1)S(1)} %copy-done.30, bf16[384,512]{1,0:T(8,128)(2,1)S(1)} %get-tuple-element.63), kind=kOutput, calls=%fused_computation.49 | convolution fusion | flops 203425152 | bytes 774144 | tf_op jit(solution)/shard_map/rqk,kd->qrd/dot_general | solution.py:79
  73.5 0.9 convolution_bitcast_fusion.1
  74.5 1.3 fusion.11
  76.1 0.4 fusion.30
  77.0 1.4 fusion.77
  78.4 2.5 %convolution_convert_fusion.4 = bf16[128,8,128]{2,0,1:T(8,128)(2,1)} fusion(bf16[384,512]{1,0:T(8,128)(2,1)} %copy-done.22, f32[8,128]{1,0:T(8,128)S(1)} %get-tuple-element.50, bf16[128,8,128]{0,2,1:T(8,128)(2,1)S(1)} %bitcast.358, pred[128,384]{0,1:T(8,128)(4,1)} %pad_add_fusion, bf16[384,512]{1,0:T(8,128)(2,1)S(1)} %get-tuple-element.63), kind=kOutput, calls=%fused_computation.50 | convolution fusion | flops 203425152 | bytes 774144 | tf_op jit(solution)/shard_map/rqk,kd->qrd/dot_general | solution.py:79
  80.9 2.6 %convolution_bitcast_fusion.2 = f32[384,128]{0,1:T(8,128)} fusion(bf16[128,8,128]{0,2,1:T(8,128)(2,1)} %bitcast.379, f32[8,128]{1,0:T(8,128)S(1)} %get-tuple-element.50, bf16[128,8,128]{0,2,1:T(8,128)(2,1)S(1)} %bitcast.359, pred[128,384]{0,1:T(8,128)(4,1)} %pad_add_fusion, bf16[384,512]{1,0:T(8,128)(2,1)S(1)} %get-tuple-element.63), kind=kOutput, calls=%fused_computation.54 | convolution fusion | flops 203294080 | bytes 872448 | tf_op jit(solution)/shard_map/rqk,qrd->kd/dot_general | solution.py:99
  83.5 1.4 fusion.14
  85.1 0.4 fusion.31
  86.1 0.8 copy.245
  86.9 0.9 copy.262
  87.8 0.9 copy.244
  88.7 0.9 copy.261
  89.5 0.9 copy.243
  90.4 0.8 copy.260
  91.2 1.4 fusion.78
  92.7 2.5 %convolution_convert_fusion.5 = bf16[128,8,128]{2,0,1:T(8,128)(2,1)} fusion(bf16[384,512]{1,0:T(8,128)(2,1)} %copy-done.22, f32[8,128]{1,0:T(8,128)S(1)} %get-tuple-element.52, bf16[128,8,128]{0,2,1:T(8,128)(2,1)S(1)} %bitcast.354, pred[128,384]{0,1:T(8,128)(4,1)} %pad_add_fusion, bf16[384,512]{1,0:T(8,128)(2,1)S(1)} %get-tuple-element.63), kind=kOutput, calls=%fused_computation.51 | convolution fusion | flops 203425152 | bytes 774144 | tf_op jit(solution)/shard_map/rqk,kd->qrd/dot_general | solution.py:79
  95.2 2.6 %convolution_bitcast_fusion.3 = f32[384,128]{0,1:T(8,128)} fusion(bf16[128,8,128]{0,2,1:T(8,128)(2,1)} %bitcast.377, f32[8,128]{1,0:T(8,128)S(1)} %get-tuple-element.52, bf16[128,8,128]{0,2,1:T(8,128)(2,1)S(1)} %bitcast.355, pred[128,384]{0,1:T(8,128)(4,1)} %pad_add_fusion, bf16[384,512]{1,0:T(8,128)(2,1)S(1)} %get-tuple-element.63), kind=kOutput, calls=%fused_computation.55 | convolution fusion | flops 203294080 | bytes 872448 | tf_op jit(solution)/shard_map/rqk,qrd->kd/dot_general | solution.py:99
  97.8 2.0 %copy.242 = bf16[1,128,1024]{2,1,0:T(8,128)(2,1)} copy(bf16[1,128,1024]{1,2,0:T(8,128)(2,1)} %bitcast.376) | data formatting | bytes 524288 | tf_op jit(solution)/shard_map/concatenate | solution.py:101
  99.8 1.0 fusion.68
  100.8 0.7 fusion.73
  101.5 0.8 copy.272
  102.3 1.2 fusion.17
  103.8 0.7 copy-done.2
  104.5 0.4 fusion.32
  104.9 0.7 fusion.72
  105.8 0.7 copy.273
  106.5 3.4 %all-to-all-start.3 = ((bf16[8,2,16,512]{3,2,1,0:T(8,128)(2,1)}), bf16[8,2,16,512]{3,2,1,0:T(8,128)(2,1)S(1)}, u32[]{:S(2)}, u32[]{:S(2)}) async-start(bf16[8,2,16,512]{3,2,1,0:T(8,128)(2,1)} %copy.273), calls=%async_computation.3 | async-start | bytes 524288 | tf_op jit(solution)/shard_map/all_to_all | solution.py:165
  110.4 6.9 %all-to-all-done.3 = bf16[8,2,16,512]{3,2,1,0:T(8,128)(2,1)S(1)} async-done(((bf16[8,2,16,512]{3,2,1,0:T(8,128)(2,1)}), bf16[8,2,16,512]{3,2,1,0:T(8,128)(2,1)S(1)}, u32[]{:S(2)}, u32[]{:S(2)}) %all-to-all-start.3) | async-done | bytes 262176 | tf_op jit(solution)/shard_map/all_to_all | solution.py:165
  117.3 0.6 fusion.24
  117.9 1.6 copy.275
  119.5 6.2 %all-to-all-start.4 = ((bf16[32,1,2,16,512]{4,3,2,1,0:T(8,128)(2,1)}), bf16[32,1,2,16,512]{4,3,2,1,0:T(8,128)(2,1)S(1)}, u32[]{:S(2)}, u32[]{:S(2)}) async-start(bf16[32,1,2,16,512]{4,3,2,1,0:T(8,128)(2,1)} %copy.275), calls=%async_computation.4 | async-start | bytes 2097152 | tf_op jit(solution)/shard_map/all_to_all | solution.py:43
  125.8 2.9 %collective-permute-start.2 = (bf16[128,2,512]{0,2,1:T(8,128)(2,1)S(1)}, bf16[128,2,512]{0,2,1:T(8,128)(2,1)S(1)}, u32[]{:S(2)}, u32[]{:S(2)}) collective-permute-start(bf16[128,2,512]{0,2,1:T(8,128)(2,1)S(1)} %pad_maximum_fusion.6), channel_id=1, source_target_pairs={{1,0},{2,1},{3,2},{4,3},{5,4},{6,5},{7,6},{8,7},{9,8},{10,9},{11,1... | collective-permute-start | bytes 786440 | tf_op jit(solution)/shard_map/ppermute | solution.py:33
  128.9 1.0 pad_maximum_fusion
  130.0 1.0 pad_maximum_fusion.1
  131.1 23.9 %collective-permute-done.2 = bf16[128,2,512]{0,2,1:T(8,128)(2,1)S(1)} collective-permute-done((bf16[128,2,512]{0,2,1:T(8,128)(2,1)S(1)}, bf16[128,2,512]{0,2,1:T(8,128)(2,1)S(1)}, u32[]{:S(2)}, u32[]{:S(2)}) %collective-permute-start.2) | collective-permute-done | bytes 262176 | tf_op jit(solution)/shard_map/ppermute | solution.py:33
  155.1 1.0 copy.276
  156.1 0.8 convert_reduce_fusion
  (102 shorter events, 4.6 us)
Async XLA Ops:
  10.7 13.5 %copy-start.35 = (s32[1,128]{1,0:T(1,128)S(1)}, s32[1,128]{1,0:T(1,128)}, u32[]{:S(2)}) copy-start(s32[1,128]{1,0:T(1,128)} %param.11) | copy-start | bytes 1540
  10.7 17.4 %copy-start.23 = (bf16[1,128,2,512]{3,2,1,0:T(2,128)(2,1)S(1)}, bf16[1,128,2,512]{3,2,1,0:T(2,128)(2,1)}, u32[]{:S(2)}) copy-start(bf16[1,128,2,512]{3,2,1,0:T(2,128)(2,1)} %param.8) | copy-start | bytes 786436
  12.6 18.9 %copy-start = (bf16[1,128,4096]{2,1,0:T(8,128)(2,1)S(1)}, bf16[1,128,4096]{2,1,0:T(8,128)(2,1)}, u32[]{:S(2)}) copy-start(bf16[1,128,4096]{2,1,0:T(8,128)(2,1)} %param.7) | copy-start | bytes 3145732
  12.6 40.4 %all-to-all-start.1 = ((bf16[32,1,2,16,512]{4,3,2,1,0:T(8,128)(2,1)}), bf16[32,1,2,16,512]{4,3,2,1,0:T(8,128)(2,1)S(1)}, u32[]{:S(2)}, u32[]{:S(2)}) async-start(bf16[32,1,2,16,512]{4,3,2,1,0:T(8,128)(2,1)} %broadcast_in_dim.47), calls=%async_computation.1 | async-start | bytes 2097152 | tf_op jit(solution)/shard_map/all_to_all | solution.py:21
  24.7 22.7 %collective-permute-start.1 = (s32[128]{0:T(128)}, s32[128]{0:T(128)}, u32[]{:S(2)}, u32[]{:S(2)}) collective-permute-start(s32[128]{0:T(128)} %broadcast_add_fusion), channel_id=1, source_target_pairs={{0,1},{1,2},{2,3},{3,4},{4,5},{5,6},{6,7},{7,8},{8,9},{9,10},{10,1... | collective-permute-start | bytes 1544 | tf_op jit(solution)/shard_map/ppermute | solution.py:33
  28.1 30.0 %collective-permute-start = (bf16[128,2,512]{2,0,1:T(8,128)(2,1)S(1)}, bf16[128,2,512]{2,0,1:T(8,128)(2,1)}, u32[]{:S(2)}, u32[]{:S(2)}) collective-permute-start(bf16[128,2,512]{2,0,1:T(8,128)(2,1)S(1)} %bitcast.348), channel_id=1, source_target_pairs={{0,1},{1,2},{2,3},{3,4},{4,5},{5,6},{6,7},{7,8},{8,9},{9,10},{10,1... | collective-permute-start | bytes 786440 | tf_op jit(solution)/shard_map/ppermute | solution.py:33
  32.2 1.6 %copy-start.34 = (s32[1,64]{1,0:T(1,128)S(1)}, s32[1,64]{1,0:T(1,128)}, u32[]{:S(2)}) copy-start(s32[1,64]{1,0:T(1,128)} %param.12) | copy-start | bytes 772
  35.7 0.9 copy-start.36
  35.7 0.9 copy-start.31
  36.9 16.8 %copy-start.32 = (s32[8]{0:T(128)}, s32[8]{0:T(128)S(1)}, u32[]{:S(2)}) copy-start(s32[8]{0:T(128)S(1)} %reduce.1) | copy-start | bytes 100
  48.8 16.7 %copy-start.18 = (bf16[128,512]{1,0:T(8,128)(2,1)S(1)}, bf16[128,512]{1,0:T(8,128)(2,1)}, u32[]{:S(2)}) copy-start(bf16[128,512]{1,0:T(8,128)(2,1)} %get-tuple-element.41) | copy-start | bytes 393220
  54.5 11.1 %copy-start.5 = (bf16[128,1024]{0,1:T(8,128)(2,1)S(1)}, bf16[128,1024]{0,1:T(8,128)(2,1)}, u32[]{:S(2)}) copy-start(bf16[128,1024]{0,1:T(8,128)(2,1)} %get-tuple-element.29) | copy-start | bytes 786436
  54.5 11.1 %copy-start.29 = (pred[128,384]{0,1:T(8,128)(4,1)S(1)}, pred[128,384]{0,1:T(8,128)(4,1)}, u32[]{:S(2)}) copy-start(pred[128,384]{0,1:T(8,128)(4,1)} %pad_add_fusion) | copy-start | bytes 147460
  54.5 11.0 %all-to-all-start.2 = ((bf16[8,2,16,512]{3,2,1,0:T(8,128)(2,1)}), bf16[8,2,16,512]{3,2,1,0:T(8,128)(2,1)S(1)}, u32[]{:S(2)}, u32[]{:S(2)}) async-start(bf16[8,2,16,512]{3,2,1,0:T(8,128)(2,1)} %copy.223), calls=%async_computation.2 | async-start | bytes 524288 | tf_op jit(solution)/shard_map/all_to_all | solution.py:125
  65.5 3.2 %copy-start.22 = (bf16[384,512]{1,0:T(8,128)(2,1)}, bf16[384,512]{1,0:T(8,128)(2,1)S(1)}, u32[]{:S(2)}) copy-start(bf16[384,512]{1,0:T(8,128)(2,1)S(1)} %get-tuple-element.62) | copy-start | bytes 1179652
  69.4 1.0 copy-start.4
  69.4 0.9 copy-start.30
  71.0 2.6 %copy-start.28 = (bf16[128,1024]{0,1:T(8,128)(2,1)S(1)}, bf16[128,1024]{0,1:T(8,128)(2,1)}, u32[]{:S(2)}) copy-start(bf16[128,1024]{0,1:T(8,128)(2,1)} %get-tuple-element.26) | copy-start | bytes 786436
  74.4 25.4 %copy-start.13 = (f32[384,128]{0,1:T(8,128)}, f32[384,128]{0,1:T(8,128)S(1)}, u32[]{:S(2)}) copy-start(f32[384,128]{0,1:T(8,128)S(1)} %convolution_bitcast_fusion.1) | copy-start | bytes 589828
  76.0 1.0 copy-start.3
  85.1 1.0 copy-start.24
  85.1 2.7 %copy-start.25 = (bf16[128,8,128]{2,0,1:T(8,128)(2,1)S(1)}, bf16[128,8,128]{2,0,1:T(8,128)(2,1)}, u32[]{:S(2)}) copy-start(bf16[128,8,128]{2,0,1:T(8,128)(2,1)} %convolution_convert_fusion.3) | copy-start | bytes 786436
  85.5 4.0 %copy-start.26 = (bf16[128,8,128]{2,0,1:T(8,128)(2,1)S(1)}, bf16[128,8,128]{2,0,1:T(8,128)(2,1)}, u32[]{:S(2)}) copy-start(bf16[128,8,128]{2,0,1:T(8,128)(2,1)} %convolution_convert_fusion.4) | copy-start | bytes 786436
  86.1 5.2 %copy-start.1 = (bf16[128,1024]{0,1:T(8,128)(2,1)S(1)}, bf16[128,1024]{0,1:T(8,128)(2,1)}, u32[]{:S(2)}) copy-start(bf16[128,1024]{0,1:T(8,128)(2,1)} %get-tuple-element.28) | copy-start | bytes 786436
  95.2 4.7 %copy-start.15 = (f32[384,128]{0,1:T(8,128)S(1)}, f32[384,128]{0,1:T(8,128)}, u32[]{:S(2)}) copy-start(f32[384,128]{0,1:T(8,128)} %convolution_bitcast_fusion.2) | copy-start | bytes 589828
  97.8 4.5 %copy-start.27 = (bf16[128,1024]{0,1:T(8,128)(2,1)S(1)}, bf16[128,1024]{0,1:T(8,128)(2,1)}, u32[]{:S(2)}) copy-start(bf16[128,1024]{0,1:T(8,128)(2,1)} %get-tuple-element.24) | copy-start | bytes 786436
  103.5 1.0 copy-start.2
  104.5 1.2 copy-start.19
  105.7 11.6 %copy-start.33 = (s32[8]{0:T(128)S(1)}, s32[8]{0:T(128)}, u32[]{:S(2)}) copy-start(s32[8]{0:T(128)} %copy-done.32) | copy-start | bytes 100
  106.5 10.9 %all-to-all-start.3 = ((bf16[8,2,16,512]{3,2,1,0:T(8,128)(2,1)}), bf16[8,2,16,512]{3,2,1,0:T(8,128)(2,1)S(1)}, u32[]{:S(2)}, u32[]{:S(2)}) async-start(bf16[8,2,16,512]{3,2,1,0:T(8,128)(2,1)} %copy.273), calls=%async_computation.3 | async-start | bytes 524288 | tf_op jit(solution)/shard_map/all_to_all | solution.py:165
  119.5 6.3 %copy-start.20 = (bf16[128,1,512]{0,2,1:T(8,128)(2,1)S(1)}, bf16[128,1,512]{0,2,1:T(8,128)(2,1)}, u32[]{:S(2)}) copy-start(bf16[128,1,512]{0,2,1:T(8,128)(2,1)} %get-tuple-element.35) | copy-start | bytes 393220
  119.5 6.3 %copy-start.21 = (bf16[128,1,512]{0,2,1:T(8,128)(2,1)S(1)}, bf16[128,1,512]{0,2,1:T(8,128)(2,1)}, u32[]{:S(2)}) copy-start(bf16[128,1,512]{0,2,1:T(8,128)(2,1)} %get-tuple-element.33) | copy-start | bytes 393220
  119.5 9.2 %copy-start.14 = (f32[384,128]{0,1:T(8,128)S(1)}, f32[384,128]{0,1:T(8,128)}, u32[]{:S(2)}) copy-start(f32[384,128]{0,1:T(8,128)} %copy-done.13) | copy-start | bytes 589828
  119.5 9.2 %copy-start.16 = (f32[384,128]{0,1:T(8,128)S(1)}, f32[384,128]{0,1:T(8,128)}, u32[]{:S(2)}) copy-start(f32[384,128]{0,1:T(8,128)} %convolution_bitcast_fusion.2) | copy-start | bytes 589828
  119.5 9.2 %copy-start.17 = (f32[384,128]{0,1:T(8,128)S(1)}, f32[384,128]{0,1:T(8,128)}, u32[]{:S(2)}) copy-start(f32[384,128]{0,1:T(8,128)} %convolution_bitcast_fusion.3) | copy-start | bytes 589828
  119.5 36.6 %all-to-all-start.4 = ((bf16[32,1,2,16,512]{4,3,2,1,0:T(8,128)(2,1)}), bf16[32,1,2,16,512]{4,3,2,1,0:T(8,128)(2,1)S(1)}, u32[]{:S(2)}, u32[]{:S(2)}) async-start(bf16[32,1,2,16,512]{4,3,2,1,0:T(8,128)(2,1)} %copy.275), calls=%async_computation.4 | async-start | bytes 2097152 | tf_op jit(solution)/shard_map/all_to_all | solution.py:43
  125.7 3.2 %copy-start.7 = (bf16[1,128,1024]{2,1,0:T(8,128)(2,1)S(1)}, bf16[1,128,1024]{2,1,0:T(8,128)(2,1)}, u32[]{:S(2)}) copy-start(bf16[1,128,1024]{2,1,0:T(8,128)(2,1)} %copy.245) | copy-start | bytes 786436
  125.7 3.1 %copy-start.9 = (bf16[1,128,1024]{2,1,0:T(8,128)(2,1)S(1)}, bf16[1,128,1024]{2,1,0:T(8,128)(2,1)}, u32[]{:S(2)}) copy-start(bf16[1,128,1024]{2,1,0:T(8,128)(2,1)} %copy.244) | copy-start | bytes 786436
  125.7 3.1 %copy-start.11 = (bf16[1,128,1024]{2,1,0:T(8,128)(2,1)S(1)}, bf16[1,128,1024]{2,1,0:T(8,128)(2,1)}, u32[]{:S(2)}) copy-start(bf16[1,128,1024]{2,1,0:T(8,128)(2,1)} %copy.243) | copy-start | bytes 786436
  125.7 3.1 %copy-start.12 = (bf16[1,128,1024]{2,1,0:T(8,128)(2,1)S(1)}, bf16[1,128,1024]{2,1,0:T(8,128)(2,1)}, u32[]{:S(2)}) copy-start(bf16[1,128,1024]{2,1,0:T(8,128)(2,1)} %copy.242) | copy-start | bytes 786436
  125.8 29.3 %collective-permute-start.2 = (bf16[128,2,512]{0,2,1:T(8,128)(2,1)S(1)}, bf16[128,2,512]{0,2,1:T(8,128)(2,1)S(1)}, u32[]{:S(2)}, u32[]{:S(2)}) collective-permute-start(bf16[128,2,512]{0,2,1:T(8,128)(2,1)S(1)} %pad_maximum_fusion.6), channel_id=1, source_target_pairs={{1,0},{2,1},{3,2},{4,3},{5,4},{6,5},{7,6},{8,7},{9,8},{10,9},{11,1... | collective-permute-start | bytes 786440 | tf_op jit(solution)/shard_map/ppermute | solution.py:33
  128.8 1.1 copy-start.6
  128.8 1.1 copy-start.8
  128.8 1.2 copy-start.10
where the time goes:
time: 158 us; the launch traced here: 157 us
  waiting for transfers between devices  51.8 us (33%)
  starting transfers between devices  34.6 us (22%)
  matrix products  28.6 us (18%)
  local copies, waits for them, and re-layouts  23.7 us (15%)
  blocking collectives  9.33 us (6%)
  other arithmetic  7.51 us (5%)
    ppermute x3, waiting for transfers between devices, from_behind(): return lax.ppermute(block, axis, route)  34.5 us
    all_to_all x1, starting transfers between devices, sent_to_all(): lax.all_to_all(jnp.broadcast_to(array[None], (size, *array.shape)), axis,...  11.6 us
    ppermute x3, starting transfers between devices, from_behind(): return lax.ppermute(block, axis, route)  9.63 us
    all_to_all x1, blocking collectives, on_device(): lax.all_to_all(ancestors[0, 0], 'trunk', split_axis=0, concat_axis=0, til...  9.33 us
    dot_general x4, matrix products, attend_block(): jnp.einsum('rqk,kd->qrd', weights_bf, value_part, preferred_element_type=...  9.14 us
    dot_general x4, matrix products, attend_block(): jnp.einsum('rqk,qrd->kd', weights_bf, grad_part, preferred_element_type=j...  7.06 us
    all_to_all x1, waiting for transfers between devices, on_device(): lax.all_to_all(trunk_part.astype(jnp.bfloat16), 'trunk', split_axis=0, co...  6.95 us
    all_to_all x1, waiting for transfers between devices, on_device(): lax.all_to_all(picked, 'trunk', split_axis=0, concat_axis=0, tiled=True)  6.25 us
  transfers between devices with their start and end apart: 7, of which 5 were waited for; matrix products, arithmetic and copies ran while one was open for 9% of the time, Pallas kernels for 0%

commit v1 on v0

v1 whole, which is shorter than its diff:
```python
import functools
import math

import jax
import jax.numpy as jnp
from jax import lax
from jax.experimental import pallas as pl
from jax.experimental.pallas import tpu as pltpu
from jax.sharding import PartitionSpec as P

KVH = 4
DH = 128
NEG = -1e30
LOG2E = math.log2(math.e)
MESH = pl.DeviceIdType.MESH


def attention_kernel(
    tags_ref, earlier_tags_ref, reach_ref, q_ref, g_ref, trunk_ref, earlier_ref, own_ref,
    att_ref, qg_ref, dtrunk_ref, dearlier_ref, down_ref, bias, weights, grads,
):
    rows = q_ref.shape[0]
    group = q_ref.shape[1] // DH
    depths, seg_len = trunk_ref.shape[0], trunk_ref.shape[3]
    trunk_len = depths * seg_len
    keys = trunk_len + 2 * rows
    scale = 1.0 / math.sqrt(DH)

    @pl.when(pl.program_id(0) == 0)
    def _():
        row_tags = tags_ref[...]
        squares = jnp.broadcast_to(row_tags, (rows, rows))
        column_tags = squares.T
        earlier_column = jnp.broadcast_to(earlier_tags_ref[...], (rows, rows)).T
        depth = lax.broadcasted_iota(jnp.int32, (trunk_len, rows), 0) // seg_len
        position = lax.broadcasted_iota(jnp.int32, (rows, rows), 0)
        query = lax.broadcasted_iota(jnp.int32, (rows, rows), 1)
        bias[:trunk_len] = jnp.where(depth < reach_ref[...], 0.0, NEG)
        bias[trunk_len : trunk_len + rows] = jnp.where(earlier_column == squares, 0.0, NEG)
        bias[trunk_len + rows :] = jnp.where(
            (column_tags == squares) & (position <= query), 0.0, NEG
        )

    def stacked(part):
        return jnp.concatenate(
            [trunk_ref[:, 0, part].reshape(trunk_len, DH), earlier_ref[part], own_ref[part]], axis=0
        )

    key_rows, value_rows = stacked(0), stacked(1)
    key_cols, value_cols = key_rows.T, value_rows.T
    allowed = bias[...]
    allowed = jnp.concatenate([allowed, allowed], axis=1)
    nt = (((1,), (1,)), ((), ()))

    def heads(ref, first):
        return jnp.concatenate(
            [ref[:, (first + i) * DH : (first + i + 1) * DH] for i in range(2)], axis=0
        )

    for first in range(0, group, 2):
        q2, g2 = heads(q_ref, first), heads(g_ref, first)
        scores = lax.dot_general(key_rows, q2, nt, preferred_element_type=jnp.float32) + allowed
        highest = jnp.max(scores, axis=0, keepdims=True)
        expo = jnp.exp2((scores - highest) * (scale * LOG2E))
        w = expo * (1.0 / jnp.sum(expo, axis=0, keepdims=True))
        w_bf = w.astype(jnp.bfloat16)
        gw = lax.dot_general(value_rows, g2, nt, preferred_element_type=jnp.float32)
        row_mean = jnp.sum(w * gw, axis=0, keepdims=True)
        sg = (w * (gw - row_mean)).astype(jnp.bfloat16)
        columns = slice(first * rows, (first + 2) * rows)
        weights[:, columns] = w_bf
        grads[:, columns] = sg
        out = jnp.dot(value_cols, w_bf, preferred_element_type=jnp.float32)
        dq = jnp.dot(key_cols, sg, preferred_element_type=jnp.float32) * scale
        for i in range(2):
            at = slice((first + i) * DH, (first + i + 1) * DH)
            part = slice(i * rows, (i + 1) * rows)
            att_ref[:, at] = out[:, part].T.astype(jnp.bfloat16)
            qg_ref[:, at] = dq[:, part].T.astype(jnp.bfloat16)

    def all_heads(ref):
        return jnp.concatenate([ref[:, i * DH : (i + 1) * DH] for i in range(group)], axis=0)

    dk = jnp.dot(grads[...], all_heads(q_ref), preferred_element_type=jnp.float32) * scale
    dv = jnp.dot(weights[...], all_heads(g_ref), preferred_element_type=jnp.float32)
    for part, grad in enumerate((dk, dv)):
        dtrunk_ref[:, 0, part] = (
            grad[:trunk_len].reshape(depths, seg_len, DH).astype(dtrunk_ref.dtype)
        )
        dearlier_ref[part] = grad[trunk_len : trunk_len + rows].astype(dearlier_ref.dtype)
        down_ref[part] = grad[trunk_len + rows :]


def attention(tags, earlier_tags, reach, q, g, trunk, earlier, own):
    rows, width = q.shape
    depths, heads, _, seg_len, _ = trunk.shape
    keys = depths * seg_len + 2 * rows
    wide = width // heads
    small = pl.BlockSpec((1, rows), lambda i: (0, 0))
    tall = pl.BlockSpec((rows, wide), lambda i: (0, i))
    segs = pl.BlockSpec((depths, 1, 2, seg_len, DH), lambda i: (0, i, 0, 0, 0))
    kv = pl.BlockSpec((2, rows, DH), lambda i: (0, 0, i))
    return pl.pallas_call(
        attention_kernel,
        grid=(heads,),
        in_specs=[small, small, small, tall, tall, segs, kv, kv],
        out_specs=[tall, tall, segs, kv, kv],
        out_shape=[
            jax.ShapeDtypeStruct(q.shape, jnp.bfloat16),
            jax.ShapeDtypeStruct(q.shape, jnp.bfloat16),
            jax.ShapeDtypeStruct(trunk.shape, jnp.bfloat16),
            jax.ShapeDtypeStruct(earlier.shape, jnp.bfloat16),
            jax.ShapeDtypeStruct(own.shape, jnp.float32),
        ],
        scratch_shapes=[
            pltpu.VMEM((keys, rows), jnp.float32),
            pltpu.VMEM((keys, wide), jnp.bfloat16),
            pltpu.VMEM((keys, wide), jnp.bfloat16),
        ],
        compiler_params=pltpu.CompilerParams(dimension_semantics=("arbitrary",)),
        cost_estimate=pl.CostEstimate(
            flops=12 * width * rows * keys, bytes_accessed=8 * rows * width, transcendentals=width * keys
        ),
        name="attention",
    )(tags, earlier_tags, reach, q, g, trunk, earlier, own)


def places():
    trunk, branch = lax.axis_index("trunk"), lax.axis_index("branch")
    return trunk, branch, branch // KVH, lax.rem(branch, KVH)


def served(index, trunk, z):
    return index // KVH, z * KVH + lax.rem(index, KVH)


def meet(trunk, branch, z, n_trunk, n_branch):
    barrier = pltpu.get_barrier_semaphore()

    def greet_branch(i, carry):
        pl.semaphore_signal(
            barrier, inc=1, device_id=(trunk, lax.rem(branch + i, n_branch)), device_id_type=MESH
        )
        return carry

    def greet_trunk(i, carry):
        pl.semaphore_signal(
            barrier,
            inc=1,
            device_id=(
                lax.rem(trunk + 1 + i // KVH, n_trunk),
                z * KVH + lax.rem(branch + lax.rem(i, KVH), KVH),
            ),
            device_id_type=MESH,
        )
        return carry

    lax.fori_loop(1, n_branch, greet_branch, 0)
    lax.fori_loop(0, (n_trunk - 1) * KVH, greet_trunk, 0)
    pl.semaphore_wait(barrier, n_branch - 1 + (n_trunk - 1) * KVH)


def send(source, target, send_sem, recv_sem, trunk, branch):
    pltpu.make_async_remote_copy(
        src_ref=source,
        dst_ref=target,
        send_sem=send_sem,
        recv_sem=recv_sem,
        device_id=(trunk, branch),
        device_id_type=MESH,
    ).start()


def arrived(ref, sem):
    pltpu.make_async_copy(ref, ref, sem).wait()


def to_branch(n_branch, trunk, branch, source, target, send_sem, recv_sem):
    def step(i, carry):
        other = lax.rem(branch + i, n_branch)
        send(source(other), target, send_sem, recv_sem, trunk, other)
        return carry

    lax.fori_loop(1, n_branch, step, 0)


def to_served(n_trunk, trunk, branch, z, y, source, target, send_sem, recv_sem):
    def step(i, carry):
        turn = i + 1
        t = lax.rem(trunk + turn // KVH, n_trunk)
        other = lax.rem(y + lax.rem(turn, KVH), KVH)
        send(source(t, other), target, send_sem, recv_sem, t, z * KVH + other)
        return carry

    lax.fori_loop(0, n_trunk * KVH - 1, step, 0)


def fetch_kernel(
    n_trunk, n_branch, segment_ref, asked_ref, own_ref, tags_ref,
    fetched_ref, earlier_ref, earlier_tags_ref, requests_ref,
    held, asked, wanted, staged, got, before, before_tags,
    send_sems, recv_sems, local_sems,
):
    trunk, branch, z, y = places()
    meet(trunk, branch, z, n_trunk, n_branch)
    me = trunk * KVH + y
    to_served(
        n_trunk, trunk, branch, z, y, lambda t, o: asked_ref, asked.at[me], send_sems.at[0], recv_sems.at[0]
    )
    mine = pltpu.make_async_copy(asked_ref, asked.at[me], recv_sems.at[0])
    mine.start()

    def head(at):
        return segment_ref.at[:, :, pl.ds(pl.multiple_of(at * DH, DH), DH)]

    to_branch(
        n_branch, trunk, branch, lambda b: head(lax.rem(b, KVH)), held.at[branch], send_sems.at[1], recv_sems.at[1]
    )
    pltpu.make_async_copy(head(y), held.at[branch], recv_sems.at[1]).start()
    after = lax.rem(branch + 1, n_branch)
    send(own_ref, before, send_sems.at[2], recv_sems.at[2], trunk, after)
    send(tags_ref, before_tags, send_sems.at[3], recv_sems.at[3], trunk, after)

    arrived(asked, recv_sems.at[0])
    local = pltpu.make_async_copy(asked, wanted, local_sems.at[0])
    local.start()
    local.wait()
    arrived(held, recv_sems.at[1])

    def pick(i, carry):
        staged[i] = held[wanted[i, 0, trunk]]
        return carry

    lax.fori_loop(0, n_trunk * KVH, pick, 0)
    to_served(
        n_trunk, trunk, branch, z, y, lambda t, o: staged.at[t * KVH + o], got.at[me], send_sems.at[4], recv_sems.at[4]
    )
    pltpu.make_async_copy(staged.at[me], got.at[me], recv_sems.at[4]).start()
    requests_ref[...] = asked[...]
    arrived(before, recv_sems.at[2])
    arrived(before_tags, recv_sems.at[3])
    earlier_ref[...] = before[...]
    earlier_tags_ref[...] = jnp.where(branch > 0, before_tags[...], 0)
    arrived(got, recv_sems.at[4])
    fetched_ref[...] = got[...]
    others = n_trunk * KVH - 1
    arrived(asked.at[pl.ds(0, others)], send_sems.at[0])
    arrived(held.at[pl.ds(0, n_branch - 1)], send_sems.at[1])
    arrived(own_ref, send_sems.at[2])
    arrived(tags_ref, send_sems.at[3])
    arrived(staged.at[pl.ds(0, others)], send_sems.at[4])


def fetch(n_trunk, n_branch, segment, asked, own, tags):
    n_served = n_trunk * KVH
    seg_len = segment.shape[1]
    piece = (2, seg_len, DH)
    vmem = pl.BlockSpec(memory_space=pltpu.VMEM)
    return pl.pallas_call(
        functools.partial(fetch_kernel, n_trunk, n_branch),
        in_specs=[vmem] * 4,
        out_specs=[vmem] * 4,
        out_shape=[
            jax.ShapeDtypeStruct((n_served, *piece), jnp.bfloat16),
            jax.ShapeDtypeStruct(own.shape, jnp.bfloat16),
            jax.ShapeDtypeStruct(tags.shape, jnp.int32),
            jax.ShapeDtypeStruct((n_served, *asked.shape), jnp.int32),
        ],
        scratch_shapes=[
            pltpu.VMEM((n_branch, *piece), jnp.bfloat16),
            pltpu.VMEM((n_served, *asked.shape), jnp.int32),
            pltpu.SMEM((n_served, *asked.shape), jnp.int32),
            pltpu.VMEM((n_served, *piece), jnp.bfloat16),
            pltpu.VMEM((n_served, *piece), jnp.bfloat16),
            pltpu.VMEM(own.shape, jnp.bfloat16),
            pltpu.VMEM(tags.shape, jnp.int32),
            pltpu.SemaphoreType.DMA((5,)),
            pltpu.SemaphoreType.DMA((5,)),
            pltpu.SemaphoreType.DMA((1,)),
        ],
        compiler_params=pltpu.CompilerParams(collective_id=0, has_side_effects=True),
        name="fetch",
    )(segment, asked, own, tags)


def return_kernel(
    n_trunk, n_branch, requests_ref, dtrunk_ref, dearlier_ref,
    trunk_grad_ref, from_next_ref,
    came, summed, sums, after_grad, send_sems, recv_sems,
):
    trunk, branch, z, y = places()
    meet(trunk, branch, z, n_trunk, n_branch)
    me = trunk * KVH + y
    to_served(
        n_trunk, trunk, branch, z, y, lambda t, o: dtrunk_ref.at[t * KVH + o], came.at[me], send_sems.at[0], recv_sems.at[0]
    )
    pltpu.make_async_copy(dtrunk_ref.at[me], came.at[me], recv_sems.at[0]).start()
    send(
        dearlier_ref, after_grad, send_sems.at[1], recv_sems.at[1], trunk, lax.rem(branch + n_branch - 1, n_branch)
    )
    arrived(came, recv_sems.at[0])

    def add_up(owner, carry):
        total = jnp.zeros(came.shape[1:], jnp.float32)
        for i in range(n_trunk * KVH):
            hit = jnp.where(requests_ref[i, 0, trunk] == owner, 1.0, 0.0)
            total = total + came[i].astype(jnp.float32) * hit
        summed[owner] = total.astype(jnp.bfloat16)
        return carry

    lax.fori_loop(0, n_branch, add_up, 0)
    to_branch(
        n_branch, trunk, branch, lambda b: summed.at[b], sums.at[branch], send_sems.at[2], recv_sems.at[2]
    )
    pltpu.make_async_copy(summed.at[branch], sums.at[branch], recv_sems.at[2]).start()
    arrived(after_grad, recv_sems.at[1])
    from_next_ref[...] = after_grad[...]
    arrived(sums, recv_sems.at[2])
    for head in range(KVH):
        total = sums[head].astype(jnp.float32)
        for i in range(1, n_branch // KVH):
            total = total + sums[i * KVH + head].astype(jnp.float32)
        trunk_grad_ref[:, :, head * DH : (head + 1) * DH] = total
    arrived(came.at[pl.ds(0, n_trunk * KVH - 1)], send_sems.at[0])
    arrived(dearlier_ref, send_sems.at[1])
    arrived(sums.at[pl.ds(0, n_branch - 1)], send_sems.at[2])


def give_back(n_trunk, n_branch, requests, dtrunk, dearlier):
    vmem = pl.BlockSpec(memory_space=pltpu.VMEM)
    piece = dtrunk.shape[1:]
    return pl.pallas_call(
        functools.partial(return_kernel, n_trunk, n_branch),
        in_specs=[pl.BlockSpec(memory_space=pltpu.SMEM), vmem, vmem],
        out_specs=[vmem] * 2,
        out_shape=[
            jax.ShapeDtypeStruct((*piece[:2], KVH * DH), jnp.float32),
            jax.ShapeDtypeStruct(dearlier.shape, jnp.bfloat16),
        ],
        scratch_shapes=[
            pltpu.VMEM(dtrunk.shape, jnp.bfloat16),
            pltpu.VMEM((n_branch, *piece), jnp.bfloat16),
            pltpu.VMEM((n_branch, *piece), jnp.bfloat16),
            pltpu.VMEM(dearlier.shape, jnp.bfloat16),
            pltpu.SemaphoreType.DMA((3,)),
            pltpu.SemaphoreType.DMA((3,)),
        ],
        compiler_params=pltpu.CompilerParams(collective_id=1, has_side_effects=True),
        name="give_back",
    )(requests, dtrunk, dearlier)


def on_device(queries, keys_values, out_grad, trunk_kv, branch_of, branch_reach, ancestors):
    n_trunk, n_branch = lax.axis_size("trunk"), lax.axis_size("branch")
    seg_len = trunk_kv.shape[3]
    own = jnp.moveaxis(keys_values[0], 1, 0)
    branch_ids = branch_of[0]
    tags = (branch_ids + 1)[None]
    asked = jnp.pad(ancestors[0], ((0, 0), (0, DH - n_trunk)))
    fetched, earlier, earlier_tags, requests = fetch(
        n_trunk, n_branch, trunk_kv[0, 0], asked, own, tags
    )
    reach_table = branch_reach[0]
    branch_index = jnp.arange(reach_table.shape[0], dtype=jnp.int32)
    reach_rows = jnp.sum(
        jnp.where(branch_ids[:, None] == branch_index[None, :], reach_table[None, :], 0), axis=1
    )
    attended, query_grad, dtrunk, dearlier, down = attention(
        tags,
        earlier_tags,
        reach_rows[None],
        queries[0],
        out_grad[0],
        fetched.reshape(n_trunk, KVH, 2, seg_len, DH),
        earlier,
        own,
    )
    trunk_grad, from_next = give_back(
        n_trunk, n_branch, requests, dtrunk.reshape(fetched.shape), dearlier
    )
    kv_grad = jnp.moveaxis(down + from_next.astype(jnp.float32), 0, 1)
    return (attended[None], query_grad[None], kv_grad[None], trunk_grad[None, None])


def solution(mesh):
    return jax.shard_map(
        on_device,
        mesh=mesh,
        in_specs=(
            P("trunk", "branch", None),
            P("trunk", "branch", None, None),
            P("trunk", "branch", None),
            P("trunk", "branch", None, None, None),
            P("trunk", "branch"),
            P("trunk", None),
            P("trunk", "branch", None),
        ),
        out_specs=(
            P("trunk", "branch", None),
            P("trunk", "branch", None),
            P("trunk", "branch", None, None),
            P("trunk", "branch", None, None, None),
        ),
        check_vma=False,
    )
```

time: 158 us -> 75.9 us (0.48)
  the two profiles are of different devices: /device:TPU:24 before, /device:TPU:1 now
where the time goes in v1:
time: 75.9 us; the launch traced here: 75.7 us
  Pallas kernels  67.4 us (89%)
  local copies, waits for them, and re-layouts  5.46 us (7%)
  other arithmetic  2.16 us (3%)
    pallas_call x1, Pallas kernels, fetch(): pl.pallas_call(functools.partial(fetch_kernel, n_trunk, n_branch), in_spe...  30.9 us
    pallas_call x1, Pallas kernels, give_back(): pl.pallas_call(functools.partial(return_kernel, n_trunk, n_branch), in_sp...  24.7 us
    pallas_call x1, Pallas kernels, attention(): pl.pallas_call(attention_kernel, grid=(heads,), in_specs=[small, small, s...  11.8 us
    unnamed x13, local copies, waits for them, and re-layouts  4.95 us

profile of v1, /device:TPU:1, one launch (start us, length us, event | category | flops | bytes accessed | tf_op | source)
XLA Modules:
  0.0 75.7 jit_solution(15664037175497635254)
XLA Ops:
  0.6 0.0 copy-start.2
  0.6 0.6 copy-done.2
  1.3 0.0 copy-start.3
  1.3 0.5 broadcast_add_fusion.tags_ref
  1.8 0.1 copy-done.3
  1.9 0.6 select_reduce_fusion
  2.6 0.0 copy-start.4
  2.6 0.7 copy-done.4
  3.2 0.5 pad.4.asked_ref
  3.7 1.7 %copy.16 = bf16[1,128,2,512]{3,1,2,0:T(8,128)(2,1)} copy(bf16[1,128,2,512]{3,2,1,0:T(2,128)(2,1)} %param.8) | data formatting | bytes 524288 | tf_op args[1]
  5.4 30.9 %fetch.1 = (bf16[32,2,16,128]{3,2,1,0:T(8,128)(2,1)}, bf16[2,128,512]{2,1,0:T(8,128)(2,1)}, s32[1,128]{1,0:T(1,128)}, s32[32,1,128]{2,1,0:T(1,128)}) custom-call(bf16[2,16,512]{2,1,0:T(8,128)(2,1)} %bitcast.25, s32[1,128]{1,0:T(1,128)} %pad.4.asked_ref, bf16[2,128,512]{2,1,0:T(8,128)(2,1)} %bitcast.21, s32[1,128]{1,0:T(1,128)} %broadcast_add_fusion.tags_ref), custom_call_target="tpu_custom_call" | custom-call | tf_op jit(solution)/shard_map/fetch/pallas_call | solution.py:259
  36.3 11.8 %attention.1 = (bf16[128,4096]{1,0:T(8,128)(2,1)}, bf16[128,4096]{1,0:T(8,128)(2,1)}, bf16[8,4,2,16,128]{4,3,2,1,0:T(8,128)(2,1)}, bf16[2,128,512]{2,1,0:T(8,128)(2,1)}, f32[2,128,512]{2,1,0:T(8,128)}) custom-call(s32[1,128]{1,0:T(1,128)} %broadcast_add_fusion.tags_ref, s32[1,128]{1,0:T(1,128)} %get-tuple-element.15.earlier_tags_ref, s32[1,128]{1,0:T(1,128)} %bitcast.34, ...), custom_call_target="tpu_custom_call" | custom-call | flops 2415919104 | bytes 4194304 | tf_op jit(solution)/shard_map/attention/pallas_call | solution.py:103
  48.0 0.0 copy-start
  48.1 24.7 %give_back.1 = (f32[2,16,512]{2,1,0:T(8,128)}, bf16[2,128,512]{2,1,0:T(8,128)(2,1)}) custom-call(s32[32,1,128]{2,1,0:T(1,128)} %get-tuple-element.21.requests_ref, bf16[32,2,16,128]{3,2,1,0:T(8,128)(2,1)} %bitcast.23, bf16[2,128,512]{2,1,0:T(8,128)(2,1)} %get-tuple-element.23.dearlier_ref), custom_call_target="tpu_custom_call" | custom-call | tf_op jit(solution)/shard_map/give_back/pallas_call | solution.py:332
  72.8 0.0 copy-done
  72.8 1.0 %add_bitcast_fusion = f32[1,128,2,512]{3,1,2,0:T(8,128)S(1)} fusion(f32[2,128,512]{2,1,0:T(8,128)S(1)} %copy-done, bf16[2,128,512]{2,1,0:T(8,128)(2,1)} %get-tuple-element.24), kind=kLoop, calls=%fused_computation | loop fusion | flops 262144 | bytes 1310720 | tf_op jit(solution)/shard_map/broadcast_in_dim | solution.py:382
  73.9 0.0 copy-start.1
  73.9 1.2 %copy.14 = f32[1,128,2,512]{3,2,1,0:T(2,128)} copy(f32[1,128,2,512]{3,1,2,0:T(8,128)S(1)} %add_bitcast_fusion) | data formatting | bytes 1048576
  75.1 0.0 copy-done.1
  75.1 0.6 copy.18
Async XLA Ops:
  0.6 0.7 copy-start.2
  1.3 0.7 copy-start.3
  2.6 0.7 copy-start.4
  48.0 24.8 %copy-start = (f32[2,128,512]{2,1,0:T(8,128)S(1)}, f32[2,128,512]{2,1,0:T(8,128)}, u32[]{:S(2)}) copy-start(f32[2,128,512]{2,1,0:T(8,128)} %get-tuple-element.20) | copy-start | bytes 1572868
  73.9 1.2 %copy-start.1 = (f32[2,16,512]{2,1,0:T(8,128)S(1)}, f32[2,16,512]{2,1,0:T(8,128)}, u32[]{:S(2)}) copy-start(f32[2,16,512]{2,1,0:T(8,128)} %get-tuple-element.25) | copy-start | bytes 196612

commit v2 on v0

v2 whole, which is shorter than its diff:
```python
import functools
import math

import jax
import jax.numpy as jnp
from jax import lax
from jax.experimental import pallas as pl
from jax.experimental.pallas import tpu as pltpu
from jax.sharding import PartitionSpec as P

KVH = 4
DH = 128
NEG = -1e30
SCALE = 1.0 / math.sqrt(DH)
EXP2_SCALE = SCALE * math.log2(math.e)
MESH = pl.DeviceIdType.MESH
NT = (((1,), (1,)), ((), ()))
HEADS_BEFORE_SUMS = 3


def dot(a, b):
    return jnp.dot(a, b, preferred_element_type=jnp.float32)


def dot_nt(a, b):
    return lax.dot_general(a, b, NT, preferred_element_type=jnp.float32)


def signal(semaphore, trunk, branch):
    pl.semaphore_signal(semaphore, inc=1, device_id=(trunk, branch), device_id_type=MESH)


def send(source, target, send_sem, recv_sem, trunk, branch):
    pltpu.make_async_remote_copy(
        src_ref=source,
        dst_ref=target,
        send_sem=send_sem,
        recv_sem=recv_sem,
        device_id=(trunk, branch),
        device_id_type=MESH,
    ).start()


def arrived(ref, sem):
    pltpu.make_async_copy(ref, ref, sem).wait()


def loop(first, last, body):
    def step(i, carry):
        body(i)
        return carry

    lax.fori_loop(first, last, step, 0)


def columns(head):
    return pl.ds(pl.multiple_of(head * DH, DH), DH)


def kernel(
    n_trunk, n_branch,
    q_hbm, g_hbm, own_ref, segment_ref, asked_ref, tags_ref, reach_ref,
    att_hbm, qg_hbm, kv_grad_ref, trunk_grad_ref,
    q, g, held, asked, wanted, staged, got, before, before_tags, bias, early, early_gw, stats,
    weights, grads, att, qg, dtrunk, dbefore, down, came, summed, sums, after_grad,
    load_sems, store_sems, local_sem, send_sems, recv_sems,
):
    trunk, branch = lax.axis_index("trunk"), lax.axis_index("branch")
    z, y = branch // KVH, lax.rem(branch, KVH)
    me = trunk * KVH + y
    n_served = n_trunk * KVH
    heads = q.shape[0]
    pairs = heads // 2
    per_group = pairs // KVH
    rows = q.shape[1]
    trunk_len = n_trunk * segment_ref.shape[1]
    after = lax.rem(branch + 1, n_branch)
    previous = lax.rem(branch + n_branch - 1, n_branch)

    barrier = pltpu.get_barrier_semaphore()
    loop(1, n_branch, lambda i: signal(barrier, trunk, lax.rem(branch + i, n_branch)))
    loop(
        0,
        (n_trunk - 1) * KVH,
        lambda i: signal(
            barrier, lax.rem(trunk + 1 + i // KVH, n_trunk), z * KVH + lax.rem(branch + lax.rem(i, KVH), KVH)
        ),
    )

    def load(i):
        pltpu.make_async_copy(q_hbm.at[:, columns(i)], q.at[i], load_sems.at[0]).start()
        pltpu.make_async_copy(g_hbm.at[:, columns(i)], g.at[i], load_sems.at[1]).start()

    loop(0, heads, load)

    squares = jnp.broadcast_to(tags_ref[...], (rows, rows))
    position = lax.broadcasted_iota(jnp.int32, (rows, rows), 0)
    query = lax.broadcasted_iota(jnp.int32, (rows, rows), 1)
    bias[2] = jnp.where((squares.T == squares) & (position <= query), 0.0, NEG)
    branches = reach_ref.shape[1]
    reach_column = jnp.broadcast_to(reach_ref[...].astype(jnp.float32), (branches, branches)).T
    branch_index = lax.broadcasted_iota(jnp.int32, (branches, rows), 0)
    reach = jnp.sum(
        jnp.where(branch_index == tags_ref[...], reach_column[:, :1], 0.0), axis=0, keepdims=True
    )
    depth = lax.broadcasted_iota(jnp.int32, (trunk_len, rows), 0) // segment_ref.shape[1]
    bias[0] = jnp.where(depth.astype(jnp.float32) < reach, 0.0, NEG)

    pl.semaphore_wait(barrier, n_branch - 1 + (n_trunk - 1) * KVH)

    def to_served(source, target, send_sem, recv_sem):
        def step(i):
            t = lax.rem(trunk + i // KVH, n_trunk)
            other = lax.rem(y + lax.rem(i, KVH), KVH)
            send(source(t, other), target, send_sem, recv_sem, t, z * KVH + other)

        loop(1, n_served, step)
        pltpu.make_async_copy(source(trunk, y), target, recv_sem).start()

    def to_branch(source, target, send_sem, recv_sem):
        def step(i):
            other = lax.rem(branch + i, n_branch)
            send(source(other), target, send_sem, recv_sem, trunk, other)

        loop(1, n_branch, step)
        pltpu.make_async_copy(source(branch), target, recv_sem).start()

    to_served(lambda t, o: asked_ref, asked.at[me], send_sems.at[0], recv_sems.at[0])
    to_branch(
        lambda b: segment_ref.at[:, :, columns(lax.rem(b, KVH))],
        held.at[branch],
        send_sems.at[1],
        recv_sems.at[1],
    )
    send(own_ref, before, send_sems.at[2], recv_sems.at[2], trunk, after)
    send(tags_ref, before_tags, send_sems.at[3], recv_sems.at[3], trunk, after)

    def two_heads(ref, pair):
        return ref[pl.ds(2 * pair, 2)].reshape(2 * rows, DH)

    def twice(part):
        return jnp.concatenate([bias[part], bias[part]], axis=1)

    def start_part(part, pair, keys, values):
        scores = dot_nt(keys, two_heads(q, pair)) + twice(part)
        highest = jnp.max(scores, axis=0, keepdims=True)
        expo = jnp.exp2((scores - highest) * EXP2_SCALE)
        gw = dot_nt(values, two_heads(g, pair))
        total = jnp.sum(expo, axis=0, keepdims=True)
        mean = jnp.sum(expo * gw, axis=0, keepdims=True)
        return expo, gw, highest, total, mean

    def start_early(part, kv):
        def group(head):
            keys, values = kv[head, 0], kv[head, 1]
            for i in range(per_group):
                pair = head * per_group + i
                expo, gw, *rest = start_part(part + 1, pair, keys, values)
                early[part, pair] = expo
                early_gw[part, pair] = gw
                for k in range(3):
                    stats[pair, 3 * part + k : 3 * part + k + 1] = rest[k]

        loop(0, KVH, group)

    arrived(q, load_sems.at[0])
    arrived(g, load_sems.at[1])
    start_early(1, own_ref)

    arrived(asked, recv_sems.at[0])
    local = pltpu.make_async_copy(asked, wanted, local_sem)
    local.start()
    local.wait()
    arrived(held, recv_sems.at[1])

    def pick(i):
        staged[i] = held[wanted[i, 0, trunk]]

    loop(0, n_served, pick)
    to_served(
        lambda t, o: staged.at[t * KVH + o], got.at[y, trunk], send_sems.at[4], recv_sems.at[4]
    )

    arrived(before_tags, recv_sems.at[3])
    earlier_tags = jnp.where(branch > 0, before_tags[...], -1)
    bias[1] = jnp.where(jnp.broadcast_to(earlier_tags, (rows, rows)).T == squares, 0.0, NEG)
    arrived(before, recv_sems.at[2])
    start_early(0, before)

    arrived(got, recv_sems.at[4])

    def fetched(head, part):
        return got[head, :, part].reshape(trunk_len, DH)

    def all_pairs(ref, head):
        return jnp.concatenate([ref[head * per_group + i] for i in range(per_group)], axis=1)

    def all_heads(ref, head):
        return ref[pl.ds(head * 2 * per_group, 2 * per_group)].reshape(2 * per_group * rows, DH)

    def trunk_group(head):
        keys, values = fetched(head, 0), fetched(head, 1)
        for i in range(per_group):
            pair = head * per_group + i
            expo, gw, highest, total, mean = start_part(0, pair, keys, values)
            best = jnp.maximum(highest, jnp.maximum(stats[pair, 0:1], stats[pair, 3:4]))
            factors = [jnp.exp2((m - best) * EXP2_SCALE) for m in (stats[pair, 0:1], stats[pair, 3:4], highest)]
            totals = (stats[pair, 1:2], stats[pair, 4:5], total)
            means = (stats[pair, 2:3], stats[pair, 5:6], mean)
            norm = 1.0 / sum(f * t for f, t in zip(factors, totals))
            factors = [f * norm for f in factors]
            row_mean = sum(f * t for f, t in zip(factors, means))
            stats[pair, 0:1] = factors[0]
            stats[pair, 1:2] = factors[1]
            stats[pair, 2:3] = row_mean
            w = expo * factors[2]
            weights[pair] = w.astype(jnp.bfloat16)
            grads[pair] = (w * (gw - row_mean)).astype(jnp.bfloat16)
        dk = dot(all_pairs(grads, head), all_heads(q, head)) * SCALE
        dv = dot(all_pairs(weights, head), all_heads(g, head))
        for part, grad in enumerate((dk, dv)):
            dtrunk[head, :, part] = grad.reshape(n_trunk, -1, DH).astype(jnp.bfloat16)

        def give(i):
            t = lax.rem(trunk + i, n_trunk)
            send(dtrunk.at[head, t], came.at[me], send_sems.at[5], recv_sems.at[5], t, z * KVH + head)

        @pl.when(head != y)
        def _():
            give(0)

        @pl.when(head == y)
        def _():
            pltpu.make_async_copy(dtrunk.at[head, trunk], came.at[me], recv_sems.at[5]).start()

        loop(1, n_trunk, give)

    loop(0, KVH, trunk_group)

    def rest_group(head):
        key_cols = jnp.concatenate([fetched(head, 0), before[head, 0], own_ref[head, 0]], axis=0).T
        value_cols = jnp.concatenate([fetched(head, 1), before[head, 1], own_ref[head, 1]], axis=0).T
        w_parts, sg_parts = [], []
        for i in range(per_group):
            pair = head * per_group + i
            row_mean = stats[pair, 2:3]
            w_bf, sg = [], []
            for part in range(2):
                w = early[part, pair] * stats[pair, part : part + 1]
                w_bf.append(w.astype(jnp.bfloat16))
                sg.append((w * (early_gw[part, pair] - row_mean)).astype(jnp.bfloat16))
            w_bf, sg = jnp.concatenate(w_bf, axis=0), jnp.concatenate(sg, axis=0)
            w_parts.append(w_bf)
            sg_parts.append(sg)
            out = dot(value_cols, jnp.concatenate([weights[pair], w_bf], axis=0))
            dq = dot(key_cols, jnp.concatenate([grads[pair], sg], axis=0)) * SCALE
            for k in range(2):
                half = slice(k * rows, (k + 1) * rows)
                att[2 * pair + k] = out[:, half].T.astype(jnp.bfloat16)
                qg[2 * pair + k] = dq[:, half].T.astype(jnp.bfloat16)
        dk = dot(jnp.concatenate(sg_parts, axis=1), all_heads(q, head)) * SCALE
        dv = dot(jnp.concatenate(w_parts, axis=1), all_heads(g, head))
        for part, grad in enumerate((dk, dv)):
            dbefore[head, part] = grad[:rows].astype(jnp.bfloat16)
            down[head, part] = grad[rows:]
        send(dbefore.at[head], after_grad.at[head], send_sems.at[6], recv_sems.at[6], trunk, previous)

        def store(i):
            at = head * 2 * per_group + i
            pltpu.make_async_copy(att.at[at], att_hbm.at[:, columns(at)], store_sems.at[0]).start()
            pltpu.make_async_copy(qg.at[at], qg_hbm.at[:, columns(at)], store_sems.at[1]).start()

        loop(0, 2 * per_group, store)

    loop(0, HEADS_BEFORE_SUMS, rest_group)

    arrived(came, recv_sems.at[5])

    def add_up(owner):
        total = jnp.zeros(came.shape[1:], jnp.float32)
        for i in range(n_served):
            hit = jnp.where(wanted[i, 0, trunk] == owner, 1.0, 0.0)
            total = total + came[i].astype(jnp.float32) * hit
        summed[owner] = total.astype(jnp.bfloat16)

    loop(0, n_branch, add_up)
    to_branch(lambda b: summed.at[b], sums.at[branch], send_sems.at[7], recv_sems.at[7])

    loop(HEADS_BEFORE_SUMS, KVH, rest_group)

    arrived(after_grad, recv_sems.at[6])

    def finish(head):
        kv_grad_ref[head] = down[head] + after_grad[head].astype(jnp.float32)

    loop(0, KVH, finish)
    arrived(sums, recv_sems.at[7])
    for head in range(KVH):
        total = sums[head].astype(jnp.float32)
        for i in range(1, n_branch // KVH):
            total = total + sums[i * KVH + head].astype(jnp.float32)
        trunk_grad_ref[:, :, head * DH : (head + 1) * DH] = total

    others = pl.ds(0, n_served - 1)
    arrived(asked.at[others], send_sems.at[0])
    arrived(held.at[pl.ds(0, n_branch - 1)], send_sems.at[1])
    arrived(own_ref, send_sems.at[2])
    arrived(tags_ref, send_sems.at[3])
    arrived(staged.at[others], send_sems.at[4])
    arrived(came.at[others], send_sems.at[5])
    arrived(dbefore, send_sems.at[6])
    arrived(sums.at[pl.ds(0, n_branch - 1)], send_sems.at[7])
    arrived(att, store_sems.at[0])
    arrived(qg, store_sems.at[1])


def fused(n_trunk, n_branch, queries, out_grad, own, segment, asked, tags, reach):
    rows, width = queries.shape
    n_served = n_trunk * KVH
    heads = width // DH
    piece = (2, segment.shape[1], DH)
    trunk_len = n_trunk * segment.shape[1]
    vmem = pl.BlockSpec(memory_space=pltpu.VMEM)
    anywhere = pl.BlockSpec(memory_space=pl.ANY)
    bf16, f32 = jnp.bfloat16, jnp.float32
    return pl.pallas_call(
        functools.partial(kernel, n_trunk, n_branch),
        in_specs=[anywhere] * 2 + [vmem] * 5,
        out_specs=[anywhere] * 2 + [vmem] * 2,
        out_shape=[
            jax.ShapeDtypeStruct(queries.shape, bf16),
            jax.ShapeDtypeStruct(queries.shape, bf16),
            jax.ShapeDtypeStruct(own.shape, f32),
            jax.ShapeDtypeStruct(segment.shape, f32),
        ],
        scratch_shapes=[
            pltpu.VMEM((heads, rows, DH), bf16),
            pltpu.VMEM((heads, rows, DH), bf16),
            pltpu.VMEM((n_branch, *piece), bf16),
            pltpu.VMEM((n_served, *asked.shape), jnp.int32),
            pltpu.SMEM((n_served, *asked.shape), jnp.int32),
            pltpu.VMEM((n_served, *piece), bf16),
            pltpu.VMEM((KVH, n_trunk, *piece), bf16),
            pltpu.VMEM(own.shape, bf16),
            pltpu.VMEM(tags.shape, jnp.int32),
            pltpu.VMEM((3, rows, rows), f32),
            pltpu.VMEM((2, heads // 2, rows, 2 * rows), f32),
            pltpu.VMEM((2, heads // 2, rows, 2 * rows), f32),
            pltpu.VMEM((heads // 2, 8, 2 * rows), f32),
            pltpu.VMEM((heads // 2, trunk_len, 2 * rows), bf16),
            pltpu.VMEM((heads // 2, trunk_len, 2 * rows), bf16),
            pltpu.VMEM((heads, rows, DH), bf16),
            pltpu.VMEM((heads, rows, DH), bf16),
            pltpu.VMEM((KVH, n_trunk, *piece), bf16),
            pltpu.VMEM(own.shape, bf16),
            pltpu.VMEM(own.shape, f32),
            pltpu.VMEM((n_served, *piece), bf16),
            pltpu.VMEM((n_branch, *piece), bf16),
            pltpu.VMEM((n_branch, *piece), bf16),
            pltpu.VMEM(own.shape, bf16),
            pltpu.SemaphoreType.DMA((2,)),
            pltpu.SemaphoreType.DMA((2,)),
            pltpu.SemaphoreType.DMA,
            pltpu.SemaphoreType.DMA((8,)),
            pltpu.SemaphoreType.DMA((8,)),
        ],
        compiler_params=pltpu.CompilerParams(collective_id=0, has_side_effects=True),
        name="tree_attention",
    )(queries, out_grad, own, segment, asked, tags, reach)


def on_device(queries, keys_values, out_grad, trunk_kv, branch_of, branch_reach, ancestors):
    n_trunk, n_branch = lax.axis_size("trunk"), lax.axis_size("branch")
    rows, _, width = keys_values.shape[1:]
    own = keys_values[0].reshape(rows, 2, KVH, DH).transpose(2, 1, 0, 3)
    asked = jnp.pad(ancestors[0], ((0, 0), (0, DH - n_trunk)))
    attended, query_grad, kv_grad, trunk_grad = fused(
        n_trunk, n_branch, queries[0], out_grad[0], own, trunk_kv[0, 0], asked, branch_of, branch_reach
    )
    kv_grad = kv_grad.transpose(2, 1, 0, 3).reshape(rows, 2, width)
    return (attended[None], query_grad[None], kv_grad[None], trunk_grad[None, None])


def solution(mesh):
    return jax.shard_map(
        on_device,
        mesh=mesh,
        in_specs=(
            P("trunk", "branch", None),
            P("trunk", "branch", None, None),
            P("trunk", "branch", None),
            P("trunk", "branch", None, None, None),
            P("trunk", "branch"),
            P("trunk", None),
            P("trunk", "branch", None),
        ),
        out_specs=(
            P("trunk", "branch", None),
            P("trunk", "branch", None),
            P("trunk", "branch", None, None),
            P("trunk", "branch", None, None, None),
        ),
        check_vma=False,
    )
```

time: 158 us -> 62.5 us (0.40)
  the two profiles are of different devices: /device:TPU:24 before, /device:TPU:1 now
where the time goes in v2:
time: 62.5 us; the launch traced here: 62.2 us
  Pallas kernels  52.9 us (85%)
  local copies, waits for them, and re-layouts  8.69 us (14%)
  between operations  0.67 us (1%)
    pallas_call x1, Pallas kernels, fused(): pl.pallas_call(functools.partial(kernel, n_trunk, n_branch), in_specs=[an...  52.9 us
    unnamed x13, local copies, waits for them, and re-layouts  6 us
    transpose x1, local copies, waits for them, and re-layouts, on_device(): kv_grad = kv_grad.transpose(2, 1, 0, 3).reshape(rows, 2, width)  1.32 us

profile of v2, /device:TPU:1, one launch (start us, length us, event | category | flops | bytes accessed | tf_op | source)
XLA Modules:
  0.0 62.2 jit_solution(14120795664447808389)
XLA Ops:
  0.6 0.0 copy-start.3
  0.6 0.6 %copy-done.3 = s32[1,1,8]{2,1,0:T(1,128)S(1)} copy-done((s32[1,1,8]{2,1,0:T(1,128)S(1)}, s32[1,1,8]{2,1,0:T(1,128)}, u32[]{:S(2)}) %copy-start.3) | copy-done | bytes 56
  1.3 0.5 pad.4.asked_ref
  1.8 1.1 %copy.11 = bf16[1,128,2,512]{1,3,2,0:T(8,128)(2,1)S(1)} copy(bf16[1,128,2,512]{3,2,1,0:T(2,128)(2,1)} %param.8) | data formatting | bytes 524288 | tf_op args[1]
  3.0 0.9 %copy.12 = bf16[128,2,4,128]{3,0,1,2:T(8,128)(2,1)} copy(bf16[128,2,4,128]{0,3,2,1:T(8,128)(2,1)S(1)} %bitcast.17) | data formatting | bytes 524288 | tf_op jit(solution)/shard_map/reshape;squeeze | solution.py:375
  3.8 52.9 %tree_attention.1 = (bf16[128,4096]{1,0:T(8,128)(2,1)}, bf16[128,4096]{1,0:T(8,128)(2,1)}, f32[4,2,128,128]{3,2,1,0:T(8,128)}, f32[2,16,512]{2,1,0:T(8,128)}) custom-call(bf16[128,4096]{1,0:T(8,128)(2,1)} %bitcast.12, bf16[128,4096]{1,0:T(8,128)(2,1)} %bitcast.13, bf16[4,2,128,128]{3,2,1,0:T(8,128)(2,1)} %bitcast.14, bf16[2,16,512]{2,1,0:T(8,128)(2,1)} %bitcast.20, ...), custom_call_target="tpu_custom_call" | custom-call | tf_op jit(solution)/shard_map/tree_attention/pallas_call | solution.py:326
  56.7 0.0 copy-start.1
  56.7 1.3 %copy.13 = f32[128,2,4,128]{0,3,2,1:T(8,128)S(1)} copy(f32[128,2,4,128]{3,0,1,2:T(8,128)} %bitcast.18) | data formatting | bytes 1048576 | tf_op jit(solution)/shard_map/transpose | solution.py:380
  58.0 1.0 %copy.14 = f32[1,128,2,512]{3,2,1,0:T(2,128)} copy(f32[1,128,2,512]{1,3,2,0:T(8,128)S(1)} %bitcast.11) | data formatting | bytes 1048576
  59.0 0.0 copy-done.1
  59.0 0.0 copy-start
  59.0 1.0 %copy.18 = bf16[1,128,4096]{2,1,0:T(8,128)(2,1)} copy(bf16[1,128,4096]{2,1,0:T(8,128)(2,1)S(1)} %bitcast.16) | data formatting | bytes 2097152
  60.0 0.6 %copy-done = bf16[128,4096]{1,0:T(8,128)(2,1)S(1)} copy-done((bf16[128,4096]{1,0:T(8,128)(2,1)S(1)}, bf16[128,4096]{1,0:T(8,128)(2,1)}, u32[]{:S(2)}) %copy-start) | copy-done | bytes 1048600
  60.6 0.0 copy-start.2
  60.6 1.0 %copy.19 = bf16[1,128,4096]{2,1,0:T(8,128)(2,1)} copy(bf16[1,128,4096]{2,1,0:T(8,128)(2,1)S(1)} %bitcast.15) | data formatting | bytes 2097152
  61.6 0.0 copy-done.2
  61.6 0.6 %copy.20 = f32[1,1,2,16,512]{4,3,2,1,0:T(8,128)} copy(f32[1,1,2,16,512]{4,3,2,1,0:T(8,128)S(1)} %bitcast.19) | data formatting | bytes 131072
Async XLA Ops:
  0.6 0.7 %copy-start.3 = (s32[1,1,8]{2,1,0:T(1,128)S(1)}, s32[1,1,8]{2,1,0:T(1,128)}, u32[]{:S(2)}) copy-start(s32[1,1,8]{2,1,0:T(1,128)} %param.13) | copy-start | bytes 100
  56.7 2.3 %copy-start.1 = (bf16[128,4096]{1,0:T(8,128)(2,1)S(1)}, bf16[128,4096]{1,0:T(8,128)(2,1)}, u32[]{:S(2)}) copy-start(bf16[128,4096]{1,0:T(8,128)(2,1)} %get-tuple-element.8) | copy-start | bytes 3145732
  59.0 1.6 %copy-start = (bf16[128,4096]{1,0:T(8,128)(2,1)S(1)}, bf16[128,4096]{1,0:T(8,128)(2,1)}, u32[]{:S(2)}) copy-start(bf16[128,4096]{1,0:T(8,128)(2,1)} %get-tuple-element.9) | copy-start | bytes 3145732
  60.6 1.0 %copy-start.2 = (f32[2,16,512]{2,1,0:T(8,128)S(1)}, f32[2,16,512]{2,1,0:T(8,128)}, u32[]{:S(2)}) copy-start(f32[2,16,512]{2,1,0:T(8,128)} %get-tuple-element.11) | copy-start | bytes 196612

commit v3 on v2

--- a/solution.py
+++ b/solution.py
@@ -15,7 +15,7 @@
 EXP2_SCALE = SCALE * math.log2(math.e)
 MESH = pl.DeviceIdType.MESH
 NT = (((1,), (1,)), ((), ()))
-HEADS_BEFORE_SUMS = 3
+HEADS_BEFORE_SUMS = 2
 
 
 def dot(a, b):
@@ -53,15 +53,26 @@
     lax.fori_loop(first, last, step, 0)
 
 
+def far_first(i, n):
+    return lax.rem(n // 2 + (i + 1) // 2 * (2 * lax.rem(i, 2) - 1) * -1 + n, n)
+
+
 def columns(head):
     return pl.ds(pl.multiple_of(head * DH, DH), DH)
 
 
+def split_up(raw, kv):
+    for part in range(2):
+        both = raw[:, part, :]
+        for head in range(KVH):
+            kv[head, part] = both[:, head * DH : (head + 1) * DH]
+
+
 def kernel(
     n_trunk, n_branch,
-    q_hbm, g_hbm, own_ref, segment_ref, asked_ref, tags_ref, reach_ref,
-    att_hbm, qg_hbm, kv_grad_ref, trunk_grad_ref,
-    q, g, held, asked, wanted, staged, got, before, before_tags, bias, early, early_gw, stats,
+    q_hbm, g_hbm, own_hbm, segment_hbm, asked_hbm, tags_hbm, reach_hbm,
+    att_out, qg_out, kv_out, trunk_out,
+    q, g, own_raw, segment_ref, asked_ref, tags_ref, reach_ref, kv_grad_ref, trunk_grad_ref, held, asked, wanted, staged, got, before_raw, own_ref, before, before_tags, bias, early, early_gw, stats,
     weights, grads, att, qg, dtrunk, dbefore, down, came, summed, sums, after_grad,
     load_sems, store_sems, local_sem, send_sems, recv_sems,
 ):
@@ -77,22 +88,46 @@
     after = lax.rem(branch + 1, n_branch)
     previous = lax.rem(branch + n_branch - 1, n_branch)
 
+    def in_branch(i):
+        dz, dy = far_first(i // KVH, n_branch // KVH), far_first(lax.rem(i, KVH), KVH)
+        return lax.rem(z + dz, n_branch // KVH) * KVH + lax.rem(y + dy, KVH)
+
+    def in_served(i):
+        dt, dy = far_first(i // KVH, n_trunk), far_first(lax.rem(i, KVH), KVH)
+        return lax.rem(trunk + dt, n_trunk), lax.rem(y + dy, KVH)
+
     barrier = pltpu.get_barrier_semaphore()
-    loop(1, n_branch, lambda i: signal(barrier, trunk, lax.rem(branch + i, n_branch)))
-    loop(
-        0,
-        (n_trunk - 1) * KVH,
-        lambda i: signal(
-            barrier, lax.rem(trunk + 1 + i // KVH, n_trunk), z * KVH + lax.rem(branch + lax.rem(i, KVH), KVH)
-        ),
-    )
+    loop(0, n_branch - 1, lambda i: signal(barrier, trunk, in_branch(i)))
+
+    def greet(i):
+        t, other = in_served(i)
+        signal(barrier, t, z * KVH + other)
+
+    loop(0, (n_trunk - 1) * KVH, greet)
 
     def load(i):
         pltpu.make_async_copy(q_hbm.at[:, columns(i)], q.at[i], load_sems.at[0]).start()
         pltpu.make_async_copy(g_hbm.at[:, columns(i)], g.at[i], load_sems.at[1]).start()
 
+    inputs = [
+        pltpu.make_async_copy(source, target, load_sems.at[2 + i])
+        for i, (source, target) in enumerate(
+            (
+                (tags_hbm, tags_ref),
+                (reach_hbm, reach_ref),
+                (asked_hbm, asked_ref),
+                (segment_hbm, segment_ref),
+                (own_hbm, own_raw),
+            )
+        )
+    ]
+    for copy in inputs:
+        copy.start()
     loop(0, heads, load)
-
+    for copy in inputs:
+        copy.wait()
+
+    split_up(own_raw, own_ref)
     squares = jnp.broadcast_to(tags_ref[...], (rows, rows))
     position = lax.broadcasted_iota(jnp.int32, (rows, rows), 0)
     query = lax.broadcasted_iota(jnp.int32, (rows, rows), 1)
@@ -110,19 +145,18 @@
 
     def to_served(source, target, send_sem, recv_sem):
         def step(i):
-            t = lax.rem(trunk + i // KVH, n_trunk)
-            other = lax.rem(y + lax.rem(i, KVH), KVH)
+            t, other = in_served(i)
             send(source(t, other), target, send_sem, recv_sem, t, z * KVH + other)
 
-        loop(1, n_served, step)
+        loop(0, n_served - 1, step)
         pltpu.make_async_copy(source(trunk, y), target, recv_sem).start()
 
     def to_branch(source, target, send_sem, recv_sem):
         def step(i):
-            other = lax.rem(branch + i, n_branch)
+            other = in_branch(i)
             send(source(other), target, send_sem, recv_sem, trunk, other)
 
-        loop(1, n_branch, step)
+        loop(0, n_branch - 1, step)
         pltpu.make_async_copy(source(branch), target, recv_sem).start()
 
     to_served(lambda t, o: asked_ref, asked.at[me], send_sems.at[0], recv_sems.at[0])
@@ -132,7 +166,7 @@
         send_sems.at[1],
         recv_sems.at[1],
     )
-    send(own_ref, before, send_sems.at[2], recv_sems.at[2], trunk, after)
+    send(own_raw, before_raw, send_sems.at[2], recv_sems.at[2], trunk, after)
     send(tags_ref, before_tags, send_sems.at[3], recv_sems.at[3], trunk, after)
 
     def two_heads(ref, pair):
@@ -184,7 +218,8 @@
     arrived(before_tags, recv_sems.at[3])
     earlier_tags = jnp.where(branch > 0, before_tags[...], -1)
     bias[1] = jnp.where(jnp.broadcast_to(earlier_tags, (rows, rows)).T == squares, 0.0, NEG)
-    arrived(before, recv_sems.at[2])
+    arrived(before_raw, recv_sems.at[2])
+    split_up(before_raw, before)
     start_early(0, before)
 
     arrived(got, recv_sems.at[4])
@@ -192,48 +227,55 @@
     def fetched(head, part):
         return got[head, :, part].reshape(trunk_len, DH)
 
-    def all_pairs(ref, head):
-        return jnp.concatenate([ref[head * per_group + i] for i in range(per_group)], axis=1)
-
     def all_heads(ref, head):
         return ref[pl.ds(head * 2 * per_group, 2 * per_group)].reshape(2 * per_group * rows, DH)
 
-    def trunk_group(head):
+    def trunk_group(turn):
+        head = lax.rem(y + far_first(turn, KVH), KVH)
         keys, values = fetched(head, 0), fetched(head, 1)
+        known = [stats[head * per_group + i] for i in range(per_group)]
+        merged, w_parts, sg_parts = [], [], []
         for i in range(per_group):
             pair = head * per_group + i
             expo, gw, highest, total, mean = start_part(0, pair, keys, values)
-            best = jnp.maximum(highest, jnp.maximum(stats[pair, 0:1], stats[pair, 3:4]))
-            factors = [jnp.exp2((m - best) * EXP2_SCALE) for m in (stats[pair, 0:1], stats[pair, 3:4], highest)]
-            totals = (stats[pair, 1:2], stats[pair, 4:5], total)
-            means = (stats[pair, 2:3], stats[pair, 5:6], mean)
+            peaks, totals, means = [
+                [known[i][k : k + 1], known[i][k + 3 : k + 4], last]
+                for k, last in enumerate((highest, total, mean))
+            ]
+            best = jnp.maximum(peaks[2], jnp.maximum(peaks[0], peaks[1]))
+            factors = [jnp.exp2((m - best) * EXP2_SCALE) for m in peaks]
             norm = 1.0 / sum(f * t for f, t in zip(factors, totals))
             factors = [f * norm for f in factors]
             row_mean = sum(f * t for f, t in zip(factors, means))
-            stats[pair, 0:1] = factors[0]
-            stats[pair, 1:2] = factors[1]
-            stats[pair, 2:3] = row_mean
+            merged.append((factors[0], factors[1], row_mean))
             w = expo * factors[2]
-            weights[pair] = w.astype(jnp.bfloat16)
-            grads[pair] = (w * (gw - row_mean)).astype(jnp.bfloat16)
-        dk = dot(all_pairs(grads, head), all_heads(q, head)) * SCALE
-        dv = dot(all_pairs(weights, head), all_heads(g, head))
+            w_parts.append(w.astype(jnp.bfloat16))
+            sg_parts.append((w * (gw - row_mean)).astype(jnp.bfloat16))
+        dv = dot(jnp.concatenate(w_parts, axis=1), all_heads(g, head))
+        dk = dot(jnp.concatenate(sg_parts, axis=1), all_heads(q, head)) * SCALE
         for part, grad in enumerate((dk, dv)):
             dtrunk[head, :, part] = grad.reshape(n_trunk, -1, DH).astype(jnp.bfloat16)
 
         def give(i):
-            t = lax.rem(trunk + i, n_trunk)
+            t = lax.rem(trunk + far_first(i, n_trunk), n_trunk)
             send(dtrunk.at[head, t], came.at[me], send_sems.at[5], recv_sems.at[5], t, z * KVH + head)
+
+        loop(0, n_trunk - 1, give)
 
         @pl.when(head != y)
         def _():
-            give(0)
+            give(n_trunk - 1)
 
         @pl.when(head == y)
         def _():
             pltpu.make_async_copy(dtrunk.at[head, trunk], came.at[me], recv_sems.at[5]).start()
 
-        loop(1, n_trunk, give)
+        for i in range(per_group):
+            pair = head * per_group + i
+            for k in range(3):
+                stats[pair, k : k + 1] = merged[i][k]
+            weights[pair] = w_parts[i]
+            grads[pair] = sg_parts[i]
 
     loop(0, KVH, trunk_group)
 
@@ -267,8 +309,8 @@
 
         def store(i):
             at = head * 2 * per_group + i
-            pltpu.make_async_copy(att.at[at], att_hbm.at[:, columns(at)], store_sems.at[0]).start()
-            pltpu.make_async_copy(qg.at[at], qg_hbm.at[:, columns(at)], store_sems.at[1]).start()
+            pltpu.make_async_copy(att.at[at], att_out.at[:, columns(at)], store_sems.at[0]).start()
+            pltpu.make_async_copy(qg.at[at], qg_out.at[:, columns(at)], store_sems.at[1]).start()
 
         loop(0, 2 * per_group, store)
 
@@ -294,6 +336,8 @@
         kv_grad_ref[head] = down[head] + after_grad[head].astype(jnp.float32)
 
     loop(0, KVH, finish)
+    kv_copy = pltpu.make_async_copy(kv_grad_ref, kv_out, store_sems.at[2])
+    kv_copy.start()
     arrived(sums, recv_sems.at[7])
     for head in range(KVH):
         total = sums[head].astype(jnp.float32)
@@ -301,10 +345,12 @@
             total = total + sums[i * KVH + head].astype(jnp.float32)
         trunk_grad_ref[:, :, head * DH : (head + 1) * DH] = total
 
+    trunk_copy = pltpu.make_async_copy(trunk_grad_ref, trunk_out, store_sems.at[3])
+    trunk_copy.start()
     others = pl.ds(0, n_served - 1)
     arrived(asked.at[others], send_sems.at[0])
     arrived(held.at[pl.ds(0, n_branch - 1)], send_sems.at[1])
-    arrived(own_ref, send_sems.at[2])
+    arrived(own_raw, send_sems.at[2])
     arrived(tags_ref, send_sems.at[3])
     arrived(staged.at[others], send_sems.at[4])
     arrived(came.at[others], send_sems.at[5])
@@ -312,6 +358,8 @@
     arrived(sums.at[pl.ds(0, n_branch - 1)], send_sems.at[7])
     arrived(att, store_sems.at[0])
     arrived(qg, store_sems.at[1])
+    kv_copy.wait()
+    trunk_copy.wait()
 
 
 def fused(n_trunk, n_branch, queries, out_grad, own, segment, asked, tags, reach):
@@ -320,28 +368,33 @@
     heads = width // DH
     piece = (2, segment.shape[1], DH)
     trunk_len = n_trunk * segment.shape[1]
-    vmem = pl.BlockSpec(memory_space=pltpu.VMEM)
+    by_head = (KVH, 2, rows, DH)
     anywhere = pl.BlockSpec(memory_space=pl.ANY)
     bf16, f32 = jnp.bfloat16, jnp.float32
     return pl.pallas_call(
         functools.partial(kernel, n_trunk, n_branch),
-        in_specs=[anywhere] * 2 + [vmem] * 5,
-        out_specs=[anywhere] * 2 + [vmem] * 2,
+        in_specs=[pl.BlockSpec(memory_space=pltpu.HBM)] * 7,
+        out_specs=[anywhere] * 4,
         out_shape=[
             jax.ShapeDtypeStruct(queries.shape, bf16),
             jax.ShapeDtypeStruct(queries.shape, bf16),
-            jax.ShapeDtypeStruct(own.shape, f32),
+            jax.ShapeDtypeStruct(by_head, f32),
             jax.ShapeDtypeStruct(segment.shape, f32),
         ],
         scratch_shapes=[
             pltpu.VMEM((heads, rows, DH), bf16),
             pltpu.VMEM((heads, rows, DH), bf16),
+            *[pltpu.VMEM(a.shape, a.dtype) for a in (own, segment, asked, tags, reach)],
+            pltpu.VMEM(by_head, f32),
+            pltpu.VMEM(segment.shape, f32),
             pltpu.VMEM((n_branch, *piece), bf16),
             pltpu.VMEM((n_served, *asked.shape), jnp.int32),
             pltpu.SMEM((n_served, *asked.shape), jnp.int32),
             pltpu.VMEM((n_served, *piece), bf16),
             pltpu.VMEM((KVH, n_trunk, *piece), bf16),
             pltpu.VMEM(own.shape, bf16),
+            pltpu.VMEM(by_head, bf16),
+            pltpu.VMEM(by_head, bf16),
             pltpu.VMEM(tags.shape, jnp.int32),
             pltpu.VMEM((3, rows, rows), f32),
             pltpu.VMEM((2, heads // 2, rows, 2 * rows), f32),
@@ -352,32 +405,71 @@
             pltpu.VMEM((heads, rows, DH), bf16),
             pltpu.VMEM((heads, rows, DH), bf16),
             pltpu.VMEM((KVH, n_trunk, *piece), bf16),
-            pltpu.VMEM(own.shape, bf16),
-            pltpu.VMEM(own.shape, f32),
+            pltpu.VMEM(by_head, bf16),
+            pltpu.VMEM(by_head, f32),
             pltpu.VMEM((n_served, *piece), bf16),
             pltpu.VMEM((n_branch, *piece), bf16),
             pltpu.VMEM((n_branch, *piece), bf16),
-            pltpu.VMEM(own.shape, bf16),
-            pltpu.SemaphoreType.DMA((2,)),
-            pltpu.SemaphoreType.DMA((2,)),
+            pltpu.VMEM(by_head, bf16),
+            pltpu.SemaphoreType.DMA((7,)),
+            pltpu.SemaphoreType.DMA((4,)),
             pltpu.SemaphoreType.DMA,
             pltpu.SemaphoreType.DMA((8,)),
             pltpu.SemaphoreType.DMA((8,)),
         ],
-        compiler_params=pltpu.CompilerParams(collective_id=0, has_side_effects=True),
+        compiler_params=pltpu.CompilerParams(
+            collective_id=0, has_side_effects=True, vmem_limit_bytes=40 << 20
+        ),
         name="tree_attention",
     )(queries, out_grad, own, segment, asked, tags, reach)
 
 
+def assemble_kernel(
+    att_in, qg_in, kv_in, trunk_in, att_out, qg_out, kv_out, trunk_out, kv, kv_rows, sems
+):
+    first = pltpu.make_async_copy(kv_in, kv, sems.at[0])
+    direct = [
+        pltpu.make_async_copy(att_in, att_out, sems.at[1]),
+        pltpu.make_async_copy(qg_in, qg_out, sems.at[2]),
+        pltpu.make_async_copy(trunk_in, trunk_out, sems.at[3]),
+    ]
+    last = pltpu.make_async_copy(kv_rows, kv_out, sems.at[4])
+    for copy in [first, *direct]:
+        copy.start()
+    first.wait()
+    for part in range(2):
+        for head in range(KVH):
+            kv_rows[:, part, head * DH : (head + 1) * DH] = kv[head, part]
+    last.start()
+    for copy in [*direct, last]:
+        copy.wait()
+
+
+def assemble(att, qg, kv_grad, trunk_grad):
+    anywhere = pl.BlockSpec(memory_space=pl.ANY)
+    heads, parts, rows, width = kv_grad.shape
+    kv_rows = jax.ShapeDtypeStruct((rows, parts, heads * width), kv_grad.dtype)
+    return pl.pallas_call(
+        assemble_kernel,
+        in_specs=[anywhere] * 4,
+        out_specs=[anywhere] * 4,
+        out_shape=[jax.ShapeDtypeStruct(a.shape, a.dtype) for a in (att, qg, kv_rows, trunk_grad)],
+        scratch_shapes=[
+            pltpu.VMEM(kv_grad.shape, kv_grad.dtype),
+            pltpu.VMEM(kv_rows.shape, kv_rows.dtype),
+            pltpu.SemaphoreType.DMA((5,)),
+        ],
+        compiler_params=pltpu.CompilerParams(vmem_limit_bytes=8 << 20),
+        name="assemble",
+    )(att, qg, kv_grad, trunk_grad)
+
+
 def on_device(queries, keys_values, out_grad, trunk_kv, branch_of, branch_reach, ancestors):
     n_trunk, n_branch = lax.axis_size("trunk"), lax.axis_size("branch")
-    rows, _, width = keys_values.shape[1:]
-    own = keys_values[0].reshape(rows, 2, KVH, DH).transpose(2, 1, 0, 3)
-    asked = jnp.pad(ancestors[0], ((0, 0), (0, DH - n_trunk)))
-    attended, query_grad, kv_grad, trunk_grad = fused(
-        n_trunk, n_branch, queries[0], out_grad[0], own, trunk_kv[0, 0], asked, branch_of, branch_reach
-    )
-    kv_grad = kv_grad.transpose(2, 1, 0, 3).reshape(rows, 2, width)
+    arrays = (queries[0], out_grad[0], keys_values[0], trunk_kv[0, 0], ancestors[0], branch_of, branch_reach)
+    arrays = [pltpu.with_memory_space_constraint(a, pltpu.HBM) for a in arrays]
+    results = fused(n_trunk, n_branch, *arrays)
+    attended, query_grad, kv_grad, trunk_grad = assemble(*results)
     return (attended[None], query_grad[None], kv_grad[None], trunk_grad[None, None])
 
 

time: 62.5 us -> 52.8 us (0.84)
  local copies, waits for them, and re-layouts: 8.69 us -> 0 us
  Pallas kernels: 52.9 us -> 52.1 us
    unnamed x13 -> x0, local copies, waits for them, and re-layouts: 6 us -> none
    transpose x1 -> x0, local copies, waits for them, and re-layouts: 1.32 us -> none  [on_device(): kv_grad = kv_grad.transpose(2, 1, 0, 3).reshape(rows, 2, width)]
    another operation x1 -> x0, local copies, waits for them, and re-layouts: 0.85 us -> none  [on_device(): own = keys_values[0].reshape(rows, 2, KVH, DH).transpose(2, 1, 0, 3)]
    pallas_call x1 -> x2, Pallas kernels: 52.9 us -> 52.1 us  [the longest x1 50.5 us: fused(): pl.pallas_call(functools.partial(kernel, n_trunk, n_branch), in_specs=[pl...]
where the time goes in v3:
time: 52.8 us; the launch traced here: 52.7 us
  Pallas kernels  52.1 us (99%)
  between operations  0.64 us (1%)
    pallas_call x1, Pallas kernels, fused(): pl.pallas_call(functools.partial(kernel, n_trunk, n_branch), in_specs=[pl...  50.5 us
    pallas_call x1, Pallas kernels, assemble(): pl.pallas_call(assemble_kernel, in_specs=[anywhere] * 4, out_specs=[anywh...  1.59 us

profile of v3, /device:TPU:1, one launch (start us, length us, event | category | flops | bytes accessed | tf_op | source)
XLA Modules:
  0.0 52.7 jit_solution(5671074755092052113)
XLA Ops:
  0.6 50.5 %tree_attention.1 = (bf16[128,4096]{1,0:T(8,128)(2,1)S(1)}, bf16[128,4096]{1,0:T(8,128)(2,1)S(1)}, f32[4,2,128,128]{3,2,1,0:T(8,128)S(1)}, f32[2,16,512]{2,1,0:T(8,128)S(1)}) custom-call(bf16[128,4096]{1,0:T(8,128)(2,1)} %bitcast.9, bf16[128,4096]{1,0:T(8,128)(2,1)} %bitcast.10, bf16[128,2,512]{2,1,0:T(2,128)(2,1)} %bitcast.11, ...), custom_call_target="tpu_custom_call" | custom-call | tf_op jit(solution)/shard_map/tree_attention/pallas_call | solution.py:374
  51.2 1.6 %assemble.1 = (bf16[128,4096]{1,0:T(8,128)(2,1)}, bf16[128,4096]{1,0:T(8,128)(2,1)}, f32[128,2,512]{2,1,0:T(2,128)}, f32[2,16,512]{2,1,0:T(8,128)}) custom-call(bf16[128,4096]{1,0:T(8,128)(2,1)S(1)} %get-tuple-element.12.att_in, bf16[128,4096]{1,0:T(8,128)(2,1)S(1)} %get-tuple-element.13.qg_in, f32[4,2,128,128]{3,2,1,0:T(8,128)S(1)} %get-tuple-element.14.kv_in, ...), custom_call_target="tpu_custom_call" | custom-call | tf_op jit(solution)/shard_map/assemble/pallas_call | solution.py:452

commit v4 on v3

--- a/solution.py
+++ b/solution.py
@@ -53,8 +53,8 @@
     lax.fori_loop(first, last, step, 0)
 
 
-def far_first(i, n):
-    return lax.rem(n // 2 + (i + 1) // 2 * (2 * lax.rem(i, 2) - 1) * -1 + n, n)
+def far_first(n):
+    return [(n // 2 + (i + 1) // 2 * (-1 if i % 2 else 1)) % n for i in range(n)]
 
 
 def columns(head):
@@ -73,7 +73,7 @@
     q_hbm, g_hbm, own_hbm, segment_hbm, asked_hbm, tags_hbm, reach_hbm,
     att_out, qg_out, kv_out, trunk_out,
     q, g, own_raw, segment_ref, asked_ref, tags_ref, reach_ref, kv_grad_ref, trunk_grad_ref, held, asked, wanted, staged, got, before_raw, own_ref, before, before_tags, bias, early, early_gw, stats,
-    weights, grads, att, qg, dtrunk, dbefore, down, came, summed, sums, after_grad,
+    weights, grads, att, qg, dtrunk, dbefore, down, came, hits, summed, sums, after_grad,
     load_sems, store_sems, local_sem, send_sems, recv_sems,
 ):
     trunk, branch = lax.axis_index("trunk"), lax.axis_index("branch")
@@ -88,44 +88,60 @@
     after = lax.rem(branch + 1, n_branch)
     previous = lax.rem(branch + n_branch - 1, n_branch)
 
-    def in_branch(i):
-        dz, dy = far_first(i // KVH, n_branch // KVH), far_first(lax.rem(i, KVH), KVH)
-        return lax.rem(z + dz, n_branch // KVH) * KVH + lax.rem(y + dy, KVH)
-
-    def in_served(i):
-        dt, dy = far_first(i // KVH, n_trunk), far_first(lax.rem(i, KVH), KVH)
-        return lax.rem(trunk + dt, n_trunk), lax.rem(y + dy, KVH)
-
-    barrier = pltpu.get_barrier_semaphore()
-    loop(0, n_branch - 1, lambda i: signal(barrier, trunk, in_branch(i)))
-
-    def greet(i):
-        t, other = in_served(i)
-        signal(barrier, t, z * KVH + other)
-
-    loop(0, (n_trunk - 1) * KVH, greet)
-
-    def load(i):
-        pltpu.make_async_copy(q_hbm.at[:, columns(i)], q.at[i], load_sems.at[0]).start()
-        pltpu.make_async_copy(g_hbm.at[:, columns(i)], g.at[i], load_sems.at[1]).start()
+    ys = [lax.rem(y + d, KVH) for d in far_first(KVH)]
+    zs = [lax.rem(z + d, n_branch // KVH) for d in far_first(n_branch // KVH)]
+    ts = [lax.rem(trunk + d, n_trunk) for d in far_first(n_trunk)]
+    in_branch = [at * KVH + other for at in zs for other in ys][:-1]
+    in_served = [(t, other) for t in ts for other in ys][:-1]
 
     inputs = [
         pltpu.make_async_copy(source, target, load_sems.at[2 + i])
         for i, (source, target) in enumerate(
             (
-                (tags_hbm, tags_ref),
-                (reach_hbm, reach_ref),
                 (asked_hbm, asked_ref),
                 (segment_hbm, segment_ref),
                 (own_hbm, own_raw),
+                (tags_hbm, tags_ref),
+                (reach_hbm, reach_ref),
             )
         )
     ]
     for copy in inputs:
         copy.start()
-    loop(0, heads, load)
+    barrier = pltpu.get_barrier_semaphore()
+    for other in in_branch:
+        signal(barrier, trunk, other)
+    for t, other in in_served[: (n_trunk - 1) * KVH]:
+        signal(barrier, t, z * KVH + other)
     for copy in inputs:
         copy.wait()
+    pl.semaphore_wait(barrier, n_branch - 1 + (n_trunk - 1) * KVH)
+
+    def to_served(source, target, send_sem, recv_sem):
+        for t, other in in_served:
+            send(source(t, other), target, send_sem, recv_sem, t, z * KVH + other)
+        pltpu.make_async_copy(source(trunk, y), target, recv_sem).start()
+
+    def to_branch(source, target, send_sem, recv_sem):
+        for other in in_branch:
+            send(source(other), target, send_sem, recv_sem, trunk, other)
+        pltpu.make_async_copy(source(branch), target, recv_sem).start()
+
+    to_served(lambda t, o: asked_ref, asked.at[me], send_sems.at[0], recv_sems.at[0])
+    to_branch(
+        lambda b: segment_ref.at[:, :, columns(lax.rem(b, KVH))],
+        held.at[branch],
+        send_sems.at[1],
+        recv_sems.at[1],
+    )
+    send(own_raw, before_raw, send_sems.at[2], recv_sems.at[2], trunk, after)
+    send(tags_ref, before_tags, send_sems.at[3], recv_sems.at[3], trunk, after)
+
+    def load(i):
+        pltpu.make_async_copy(q_hbm.at[:, columns(i)], q.at[i], load_sems.at[0]).start()
+        pltpu.make_async_copy(g_hbm.at[:, columns(i)], g.at[i], load_sems.at[1]).start()
+
+    loop(0, heads, load)
 
     split_up(own_raw, own_ref)
     squares = jnp.broadcast_to(tags_ref[...], (rows, rows))
@@ -141,34 +157,6 @@
     depth = lax.broadcasted_iota(jnp.int32, (trunk_len, rows), 0) // segment_ref.shape[1]
     bias[0] = jnp.where(depth.astype(jnp.float32) < reach, 0.0, NEG)
 
-    pl.semaphore_wait(barrier, n_branch - 1 + (n_trunk - 1) * KVH)
-
-    def to_served(source, target, send_sem, recv_sem):
-        def step(i):
-            t, other = in_served(i)
-            send(source(t, other), target, send_sem, recv_sem, t, z * KVH + other)
-
-        loop(0, n_served - 1, step)
-        pltpu.make_async_copy(source(trunk, y), target, recv_sem).start()
-
-    def to_branch(source, target, send_sem, recv_sem):
-        def step(i):
-            other = in_branch(i)
-            send(source(other), target, send_sem, recv_sem, trunk, other)
-
-        loop(0, n_branch - 1, step)
-        pltpu.make_async_copy(source(branch), target, recv_sem).start()
-
-    to_served(lambda t, o: asked_ref, asked.at[me], send_sems.at[0], recv_sems.at[0])
-    to_branch(
-        lambda b: segment_ref.at[:, :, columns(lax.rem(b, KVH))],
-        held.at[branch],
-        send_sems.at[1],
-        recv_sems.at[1],
-    )
-    send(own_raw, before_raw, send_sems.at[2], recv_sems.at[2], trunk, after)
-    send(tags_ref, before_tags, send_sems.at[3], recv_sems.at[3], trunk, after)
-
     def two_heads(ref, pair):
         return ref[pl.ds(2 * pair, 2)].reshape(2 * rows, DH)
 
@@ -205,6 +193,26 @@
     local = pltpu.make_async_copy(asked, wanted, local_sem)
     local.start()
     local.wait()
+
+    piece_rows = 2 * segment_ref.shape[1]
+    lane = lax.broadcasted_iota(jnp.int32, (piece_rows, DH), 1)
+    line = lax.broadcasted_iota(jnp.int32, (piece_rows, DH), 0)
+    diagonal = jnp.where(lax.rem(lane, piece_rows) == line, 1.0, 0.0)
+    per_tile = DH // piece_rows
+    sources = []
+    for tile in range(n_served // per_tile):
+        source = jnp.full((piece_rows, DH), wanted[tile * per_tile, 0, trunk], jnp.int32)
+        for i in range(1, per_tile):
+            source = jnp.where(lane >= i * piece_rows, wanted[tile * per_tile + i, 0, trunk], source)
+        sources.append(source)
+
+    def mark(owner):
+        for tile, source in enumerate(sources):
+            hits[owner, :, tile * DH : (tile + 1) * DH] = jnp.where(source == owner, diagonal, 0.0).astype(
+                jnp.bfloat16
+            )
+
+    loop(0, n_branch, mark)
     arrived(held, recv_sems.at[1])
 
     def pick(i):
@@ -231,7 +239,7 @@
         return ref[pl.ds(head * 2 * per_group, 2 * per_group)].reshape(2 * per_group * rows, DH)
 
     def trunk_group(turn):
-        head = lax.rem(y + far_first(turn, KVH), KVH)
+        head = lax.rem(y + KVH // 2 + lax.div(turn + 1, 2) * (1 - 2 * lax.rem(turn, 2)) + KVH, KVH)
         keys, values = fetched(head, 0), fetched(head, 1)
         known = [stats[head * per_group + i] for i in range(per_group)]
         merged, w_parts, sg_parts = [], [], []
@@ -256,15 +264,15 @@
         for part, grad in enumerate((dk, dv)):
             dtrunk[head, :, part] = grad.reshape(n_trunk, -1, DH).astype(jnp.bfloat16)
 
-        def give(i):
-            t = lax.rem(trunk + far_first(i, n_trunk), n_trunk)
+        def give(t):
             send(dtrunk.at[head, t], came.at[me], send_sems.at[5], recv_sems.at[5], t, z * KVH + head)
 
-        loop(0, n_trunk - 1, give)
+        for t in ts[:-1]:
+            give(t)
 
         @pl.when(head != y)
         def _():
-            give(n_trunk - 1)
+            give(trunk)
 
         @pl.when(head == y)
         def _():
@@ -318,24 +326,22 @@
 
     arrived(came, recv_sems.at[5])
 
-    def add_up(owner):
-        total = jnp.zeros(came.shape[1:], jnp.float32)
-        for i in range(n_served):
-            hit = jnp.where(wanted[i, 0, trunk] == owner, 1.0, 0.0)
-            total = total + came[i].astype(jnp.float32) * hit
-        summed[owner] = total.astype(jnp.bfloat16)
-
-    loop(0, n_branch, add_up)
+    all_sums = dot(
+        hits[...].reshape(n_branch * piece_rows, n_served * piece_rows),
+        came[...].reshape(n_served * piece_rows, DH),
+    )
+    summed[...] = all_sums.astype(jnp.bfloat16).reshape(summed.shape)
     to_branch(lambda b: summed.at[b], sums.at[branch], send_sems.at[7], recv_sems.at[7])
 
     loop(HEADS_BEFORE_SUMS, KVH, rest_group)
 
     arrived(after_grad, recv_sems.at[6])
 
-    def finish(head):
-        kv_grad_ref[head] = down[head] + after_grad[head].astype(jnp.float32)
-
-    loop(0, KVH, finish)
+    for part in range(2):
+        for head in range(KVH):
+            kv_grad_ref[:, part, head * DH : (head + 1) * DH] = down[head, part] + after_grad[
+                head, part
+            ].astype(jnp.float32)
     kv_copy = pltpu.make_async_copy(kv_grad_ref, kv_out, store_sems.at[2])
     kv_copy.start()
     arrived(sums, recv_sems.at[7])
@@ -378,14 +384,14 @@
         out_shape=[
             jax.ShapeDtypeStruct(queries.shape, bf16),
             jax.ShapeDtypeStruct(queries.shape, bf16),
-            jax.ShapeDtypeStruct(by_head, f32),
+            jax.ShapeDtypeStruct(own.shape, f32),
             jax.ShapeDtypeStruct(segment.shape, f32),
         ],
         scratch_shapes=[
             pltpu.VMEM((heads, rows, DH), bf16),
             pltpu.VMEM((heads, rows, DH), bf16),
             *[pltpu.VMEM(a.shape, a.dtype) for a in (own, segment, asked, tags, reach)],
-            pltpu.VMEM(by_head, f32),
+            pltpu.VMEM(own.shape, f32),
             pltpu.VMEM(segment.shape, f32),
             pltpu.VMEM((n_branch, *piece), bf16),
             pltpu.VMEM((n_served, *asked.shape), jnp.int32),
@@ -408,6 +414,7 @@
             pltpu.VMEM(by_head, bf16),
             pltpu.VMEM(by_head, f32),
             pltpu.VMEM((n_served, *piece), bf16),
+            pltpu.VMEM((n_branch, 2 * piece[1], n_served * 2 * piece[1]), bf16),
             pltpu.VMEM((n_branch, *piece), bf16),
             pltpu.VMEM((n_branch, *piece), bf16),
             pltpu.VMEM(by_head, bf16),
@@ -424,44 +431,26 @@
     )(queries, out_grad, own, segment, asked, tags, reach)
 
 
-def assemble_kernel(
-    att_in, qg_in, kv_in, trunk_in, att_out, qg_out, kv_out, trunk_out, kv, kv_rows, sems
-):
-    first = pltpu.make_async_copy(kv_in, kv, sems.at[0])
-    direct = [
-        pltpu.make_async_copy(att_in, att_out, sems.at[1]),
-        pltpu.make_async_copy(qg_in, qg_out, sems.at[2]),
-        pltpu.make_async_copy(trunk_in, trunk_out, sems.at[3]),
-    ]
-    last = pltpu.make_async_copy(kv_rows, kv_out, sems.at[4])
-    for copy in [first, *direct]:
+def assemble_kernel(*refs):
+    count = len(refs) // 2
+    copies = [pltpu.make_async_copy(refs[i], refs[count + i], refs[-1].at[i]) for i in range(count)]
+    for copy in copies:
         copy.start()
-    first.wait()
-    for part in range(2):
-        for head in range(KVH):
-            kv_rows[:, part, head * DH : (head + 1) * DH] = kv[head, part]
-    last.start()
-    for copy in [*direct, last]:
+    for copy in copies:
         copy.wait()
 
 
-def assemble(att, qg, kv_grad, trunk_grad):
+def assemble(*arrays):
     anywhere = pl.BlockSpec(memory_space=pl.ANY)
-    heads, parts, rows, width = kv_grad.shape
-    kv_rows = jax.ShapeDtypeStruct((rows, parts, heads * width), kv_grad.dtype)
     return pl.pallas_call(
         assemble_kernel,
-        in_specs=[anywhere] * 4,
-        out_specs=[anywhere] * 4,
-        out_shape=[jax.ShapeDtypeStruct(a.shape, a.dtype) for a in (att, qg, kv_rows, trunk_grad)],
-        scratch_shapes=[
-            pltpu.VMEM(kv_grad.shape, kv_grad.dtype),
-            pltpu.VMEM(kv_rows.shape, kv_rows.dtype),
-            pltpu.SemaphoreType.DMA((5,)),
-        ],
+        in_specs=[anywhere] * len(arrays),
+        out_specs=[anywhere] * len(arrays),
+        out_shape=[jax.ShapeDtypeStruct(a.shape, a.dtype) for a in arrays],
+        scratch_shapes=[pltpu.SemaphoreType.DMA((len(arrays),))],
         compiler_params=pltpu.CompilerParams(vmem_limit_bytes=8 << 20),
         name="assemble",
-    )(att, qg, kv_grad, trunk_grad)
+    )(*arrays)
 
 
 def on_device(queries, keys_values, out_grad, trunk_kv, branch_of, branch_reach, ancestors):

time: 52.8 us -> 50 us (0.947)
  the two profiles are of different devices: /device:TPU:1 before, /device:TPU:24 now
where the time goes in v4:
time: 50 us; the launch traced here: 49.8 us
  Pallas kernels  49.2 us (98%)
  between operations  0.64 us (1%)
    pallas_call x1, Pallas kernels, fused(): pl.pallas_call(functools.partial(kernel, n_trunk, n_branch), in_specs=[pl...  47.6 us
    pallas_call x1, Pallas kernels, assemble(): pl.pallas_call(assemble_kernel, in_specs=[anywhere] * len(arrays), out_sp...  1.53 us

profile of v4, /device:TPU:24, one launch (start us, length us, event | category | flops | bytes accessed | tf_op | source)
XLA Modules:
  0.0 49.8 jit_solution(15361886822595236046)
XLA Ops:
  0.6 47.6 %tree_attention.1 = (bf16[128,4096]{1,0:T(8,128)(2,1)S(1)}, bf16[128,4096]{1,0:T(8,128)(2,1)S(1)}, f32[128,2,512]{2,1,0:T(2,128)S(1)}, f32[2,16,512]{2,1,0:T(8,128)S(1)}) custom-call(bf16[128,4096]{1,0:T(8,128)(2,1)} %bitcast.9, bf16[128,4096]{1,0:T(8,128)(2,1)} %bitcast.10, bf16[128,2,512]{2,1,0:T(2,128)(2,1)} %bitcast.11, bf16[2,16,512]{2,1,0:T(8,128)(2,1)} %bitcast.12, ...), custom_call_target="tpu_custom_call" | custom-call | tf_op jit(solution)/shard_map/tree_attention/pallas_call | solution.py:380
  48.3 1.5 %assemble.1 = (bf16[128,4096]{1,0:T(8,128)(2,1)}, bf16[128,4096]{1,0:T(8,128)(2,1)}, f32[128,2,512]{2,1,0:T(2,128)}, f32[2,16,512]{2,1,0:T(8,128)}) custom-call(bf16[128,4096]{1,0:T(8,128)(2,1)S(1)} %get-tuple-element.12.refs_0_, bf16[128,4096]{1,0:T(8,128)(2,1)S(1)} %get-tuple-element.13.refs_1_, f32[128,2,512]{2,1,0:T(2,128)S(1)} %get-tuple-element.14.refs_2_, ...), custom_call_target="tpu_custom_call" | custom-call | tf_op jit(solution)/shard_map/assemble/pallas_call | solution.py:445

commit v5 on v4

--- a/solution.py
+++ b/solution.py
@@ -15,7 +15,7 @@
 EXP2_SCALE = SCALE * math.log2(math.e)
 MESH = pl.DeviceIdType.MESH
 NT = (((1,), (1,)), ((), ()))
-HEADS_BEFORE_SUMS = 2
+SENT_FIRST = 2
 
 
 def dot(a, b):
@@ -74,7 +74,7 @@
     att_out, qg_out, kv_out, trunk_out,
     q, g, own_raw, segment_ref, asked_ref, tags_ref, reach_ref, kv_grad_ref, trunk_grad_ref, held, asked, wanted, staged, got, before_raw, own_ref, before, before_tags, bias, early, early_gw, stats,
     weights, grads, att, qg, dtrunk, dbefore, down, came, hits, summed, sums, after_grad,
-    load_sems, store_sems, local_sem, send_sems, recv_sems,
+    load_sems, store_sems, local_sem, send_sems, recv_sems, head_sems,
 ):
     trunk, branch = lax.axis_index("trunk"), lax.axis_index("branch")
     z, y = branch // KVH, lax.rem(branch, KVH)
@@ -215,12 +215,10 @@
     loop(0, n_branch, mark)
     arrived(held, recv_sems.at[1])
 
-    def pick(i):
+    for i in range(n_served):
         staged[i] = held[wanted[i, 0, trunk]]
-
-    loop(0, n_served, pick)
     to_served(
-        lambda t, o: staged.at[t * KVH + o], got.at[y, trunk], send_sems.at[4], recv_sems.at[4]
+        lambda t, o: staged.at[t * KVH + o], got.at[y, trunk], send_sems.at[4], head_sems.at[y]
     )
 
     arrived(before_tags, recv_sems.at[3])
@@ -230,8 +228,6 @@
     split_up(before_raw, before)
     start_early(0, before)
 
-    arrived(got, recv_sems.at[4])
-
     def fetched(head, part):
         return got[head, :, part].reshape(trunk_len, DH)
 
@@ -239,7 +235,8 @@
         return ref[pl.ds(head * 2 * per_group, 2 * per_group)].reshape(2 * per_group * rows, DH)
 
     def trunk_group(turn):
-        head = lax.rem(y + KVH // 2 + lax.div(turn + 1, 2) * (1 - 2 * lax.rem(turn, 2)) + KVH, KVH)
+        head = lax.rem(y + turn, KVH)
+        arrived(got.at[head], head_sems.at[head])
         keys, values = fetched(head, 0), fetched(head, 1)
         known = [stats[head * per_group + i] for i in range(per_group)]
         merged, w_parts, sg_parts = [], [], []
@@ -282,38 +279,46 @@
             pair = head * per_group + i
             for k in range(3):
                 stats[pair, k : k + 1] = merged[i][k]
-            weights[pair] = w_parts[i]
-            grads[pair] = sg_parts[i]
+            weights[pair, :trunk_len] = w_parts[i]
+            grads[pair, :trunk_len] = sg_parts[i]
 
     loop(0, KVH, trunk_group)
 
-    def rest_group(head):
+    def final_part(part, pair):
+        known = stats[pair]
+        w = early[part, pair] * known[part : part + 1]
+        return w.astype(jnp.bfloat16), (w * (early_gw[part, pair] - known[2:3])).astype(jnp.bfloat16)
+
+    def key_grads(w_parts, sg_parts, head):
+        dk = dot(jnp.concatenate(sg_parts, axis=1), all_heads(q, head)) * SCALE
+        return dk, dot(jnp.concatenate(w_parts, axis=1), all_heads(g, head))
+
+    def before_group(head):
+        w_parts, sg_parts = zip(*[final_part(0, head * per_group + i) for i in range(per_group)])
+        for part, grad in enumerate(key_grads(w_parts, sg_parts, head)):
+            dbefore[head, part] = grad.astype(jnp.bfloat16)
+        for i in range(per_group):
+            pair = head * per_group + i
+            weights[pair, trunk_len:] = w_parts[i]
+            grads[pair, trunk_len:] = sg_parts[i]
+
+    def send_before(head):
+        send(dbefore.at[head], after_grad.at[head], send_sems.at[6], recv_sems.at[6], trunk, previous)
+
+    def own_group(head):
         key_cols = jnp.concatenate([fetched(head, 0), before[head, 0], own_ref[head, 0]], axis=0).T
         value_cols = jnp.concatenate([fetched(head, 1), before[head, 1], own_ref[head, 1]], axis=0).T
-        w_parts, sg_parts = [], []
+        w_parts, sg_parts = zip(*[final_part(1, head * per_group + i) for i in range(per_group)])
         for i in range(per_group):
             pair = head * per_group + i
-            row_mean = stats[pair, 2:3]
-            w_bf, sg = [], []
-            for part in range(2):
-                w = early[part, pair] * stats[pair, part : part + 1]
-                w_bf.append(w.astype(jnp.bfloat16))
-                sg.append((w * (early_gw[part, pair] - row_mean)).astype(jnp.bfloat16))
-            w_bf, sg = jnp.concatenate(w_bf, axis=0), jnp.concatenate(sg, axis=0)
-            w_parts.append(w_bf)
-            sg_parts.append(sg)
-            out = dot(value_cols, jnp.concatenate([weights[pair], w_bf], axis=0))
-            dq = dot(key_cols, jnp.concatenate([grads[pair], sg], axis=0)) * SCALE
+            out = dot(value_cols, jnp.concatenate([weights[pair], w_parts[i]], axis=0))
+            dq = dot(key_cols, jnp.concatenate([grads[pair], sg_parts[i]], axis=0)) * SCALE
             for k in range(2):
                 half = slice(k * rows, (k + 1) * rows)
                 att[2 * pair + k] = out[:, half].T.astype(jnp.bfloat16)
                 qg[2 * pair + k] = dq[:, half].T.astype(jnp.bfloat16)
-        dk = dot(jnp.concatenate(sg_parts, axis=1), all_heads(q, head)) * SCALE
-        dv = dot(jnp.concatenate(w_parts, axis=1), all_heads(g, head))
-        for part, grad in enumerate((dk, dv)):
-            dbefore[head, part] = grad[:rows].astype(jnp.bfloat16)
-            down[head, part] = grad[rows:]
-        send(dbefore.at[head], after_grad.at[head], send_sems.at[6], recv_sems.at[6], trunk, previous)
+        for part, grad in enumerate(key_grads(w_parts, sg_parts, head)):
+            down[head, part] = grad
 
         def store(i):
             at = head * 2 * per_group + i
@@ -322,7 +327,12 @@
 
         loop(0, 2 * per_group, store)
 
-    loop(0, HEADS_BEFORE_SUMS, rest_group)
+    def before_and_send(head):
+        before_group(head)
+        send_before(head)
+
+    loop(0, SENT_FIRST, before_and_send)
+    loop(SENT_FIRST, KVH, before_group)
 
     arrived(came, recv_sems.at[5])
 
@@ -333,7 +343,8 @@
     summed[...] = all_sums.astype(jnp.bfloat16).reshape(summed.shape)
     to_branch(lambda b: summed.at[b], sums.at[branch], send_sems.at[7], recv_sems.at[7])
 
-    loop(HEADS_BEFORE_SUMS, KVH, rest_group)
+    loop(SENT_FIRST, KVH, send_before)
+    loop(0, KVH, own_group)
 
     arrived(after_grad, recv_sems.at[6])
 
@@ -406,8 +417,8 @@
             pltpu.VMEM((2, heads // 2, rows, 2 * rows), f32),
             pltpu.VMEM((2, heads // 2, rows, 2 * rows), f32),
             pltpu.VMEM((heads // 2, 8, 2 * rows), f32),
-            pltpu.VMEM((heads // 2, trunk_len, 2 * rows), bf16),
-            pltpu.VMEM((heads // 2, trunk_len, 2 * rows), bf16),
+            pltpu.VMEM((heads // 2, trunk_len + rows, 2 * rows), bf16),
+            pltpu.VMEM((heads // 2, trunk_len + rows, 2 * rows), bf16),
             pltpu.VMEM((heads, rows, DH), bf16),
             pltpu.VMEM((heads, rows, DH), bf16),
             pltpu.VMEM((KVH, n_trunk, *piece), bf16),
@@ -423,6 +434,7 @@
             pltpu.SemaphoreType.DMA,
             pltpu.SemaphoreType.DMA((8,)),
             pltpu.SemaphoreType.DMA((8,)),
+            pltpu.SemaphoreType.DMA((KVH,)),
         ],
         compiler_params=pltpu.CompilerParams(
             collective_id=0, has_side_effects=True, vmem_limit_bytes=40 << 20

time: 50 us -> 49.2 us (0.984)
  the two profiles are of different devices: /device:TPU:24 before, /device:TPU:1 now
where the time goes in v5:
time: 49.2 us; the launch traced here: 48.9 us
  Pallas kernels  48.3 us (98%)
  between operations  0.64 us (1%)
    pallas_call x1, Pallas kernels, fused(): pl.pallas_call(functools.partial(kernel, n_trunk, n_branch), in_specs=[pl...  46.8 us
    pallas_call x1, Pallas kernels, assemble(): pl.pallas_call(assemble_kernel, in_specs=[anywhere] * len(arrays), out_sp...  1.53 us

profile of v5, /device:TPU:1, one launch (start us, length us, event | category | flops | bytes accessed | tf_op | source)
XLA Modules:
  0.0 48.9 jit_solution(16525660567841496305)
XLA Ops:
  0.6 46.8 %tree_attention.1 = (bf16[128,4096]{1,0:T(8,128)(2,1)S(1)}, bf16[128,4096]{1,0:T(8,128)(2,1)S(1)}, f32[128,2,512]{2,1,0:T(2,128)S(1)}, f32[2,16,512]{2,1,0:T(8,128)S(1)}) custom-call(bf16[128,4096]{1,0:T(8,128)(2,1)} %bitcast.9, bf16[128,4096]{1,0:T(8,128)(2,1)} %bitcast.10, bf16[128,2,512]{2,1,0:T(2,128)(2,1)} %bitcast.11, bf16[2,16,512]{2,1,0:T(8,128)(2,1)} %bitcast.12, ...), custom_call_target="tpu_custom_call" | custom-call | tf_op jit(solution)/shard_map/tree_attention/pallas_call | solution.py:391
  47.4 1.5 %assemble.1 = (bf16[128,4096]{1,0:T(8,128)(2,1)}, bf16[128,4096]{1,0:T(8,128)(2,1)}, f32[128,2,512]{2,1,0:T(2,128)}, f32[2,16,512]{2,1,0:T(8,128)}) custom-call(bf16[128,4096]{1,0:T(8,128)(2,1)S(1)} %get-tuple-element.12.refs_0_, bf16[128,4096]{1,0:T(8,128)(2,1)S(1)} %get-tuple-element.13.refs_1_, f32[128,2,512]{2,1,0:T(2,128)S(1)} %get-tuple-element.14.refs_2_, ...), custom_call_target="tpu_custom_call" | custom-call | tf_op jit(solution)/shard_map/assemble/pallas_call | solution.py:457

commit v6 on v5

--- a/solution.py
+++ b/solution.py
@@ -127,13 +127,13 @@
             send(source(other), target, send_sem, recv_sem, trunk, other)
         pltpu.make_async_copy(source(branch), target, recv_sem).start()
 
-    to_served(lambda t, o: asked_ref, asked.at[me], send_sems.at[0], recv_sems.at[0])
     to_branch(
         lambda b: segment_ref.at[:, :, columns(lax.rem(b, KVH))],
         held.at[branch],
         send_sems.at[1],
         recv_sems.at[1],
     )
+    to_served(lambda t, o: asked_ref, asked.at[me], send_sems.at[0], recv_sems.at[0])
     send(own_raw, before_raw, send_sems.at[2], recv_sems.at[2], trunk, after)
     send(tags_ref, before_tags, send_sems.at[3], recv_sems.at[3], trunk, after)
 
@@ -336,12 +336,18 @@
 
     arrived(came, recv_sems.at[5])
 
-    all_sums = dot(
-        hits[...].reshape(n_branch * piece_rows, n_served * piece_rows),
-        came[...].reshape(n_served * piece_rows, DH),
-    )
-    summed[...] = all_sums.astype(jnp.bfloat16).reshape(summed.shape)
-    to_branch(lambda b: summed.at[b], sums.at[branch], send_sems.at[7], recv_sems.at[7])
+    arrivals = came[...].reshape(n_served * piece_rows, DH)
+    half = len(zs) // 2
+    for k in range(2):
+        mine = zs[k * half : (k + 1) * half]
+        marks = [hits[pl.ds(at * KVH, KVH)].reshape(KVH * piece_rows, -1) for at in mine]
+        part = dot(jnp.concatenate(marks, axis=0), arrivals).astype(jnp.bfloat16)
+        part = part.reshape(half, KVH, *summed.shape[1:])
+        for i, at in enumerate(mine):
+            summed[pl.ds(at * KVH, KVH)] = part[i]
+        for other in in_branch[k * half * KVH : (k + 1) * half * KVH]:
+            send(summed.at[other], sums.at[branch], send_sems.at[7], recv_sems.at[7], trunk, other)
+    pltpu.make_async_copy(summed.at[branch], sums.at[branch], recv_sems.at[7]).start()
 
     loop(SENT_FIRST, KVH, send_before)
     loop(0, KVH, own_group)
@@ -445,7 +451,13 @@
 
 def assemble_kernel(*refs):
     count = len(refs) // 2
-    copies = [pltpu.make_async_copy(refs[i], refs[count + i], refs[-1].at[i]) for i in range(count)]
+    copies = []
+    for i in range(count):
+        source, target = refs[i], refs[count + i]
+        step = source.shape[0] // 2
+        for k in range(2):
+            at = pl.ds(k * step, step)
+            copies.append(pltpu.make_async_copy(source.at[at], target.at[at], refs[-1].at[i, k]))
     for copy in copies:
         copy.start()
     for copy in copies:
@@ -459,7 +471,7 @@
         in_specs=[anywhere] * len(arrays),
         out_specs=[anywhere] * len(arrays),
         out_shape=[jax.ShapeDtypeStruct(a.shape, a.dtype) for a in arrays],
-        scratch_shapes=[pltpu.SemaphoreType.DMA((len(arrays),))],
+        scratch_shapes=[pltpu.SemaphoreType.DMA((len(arrays), 2))],
         compiler_params=pltpu.CompilerParams(vmem_limit_bytes=8 << 20),
         name="assemble",
     )(*arrays)

time: 49.2 us -> 48.9 us (level)
  no operation moved by 1% of the time
where the time goes in v6:
time: 48.9 us; the launch traced here: 48.7 us
  Pallas kernels  48 us (98%)
  between operations  0.64 us (1%)
    pallas_call x1, Pallas kernels, fused(): pl.pallas_call(functools.partial(kernel, n_trunk, n_branch), in_specs=[pl...  46.5 us
    pallas_call x1, Pallas kernels, assemble(): pl.pallas_call(assemble_kernel, in_specs=[anywhere] * len(arrays), out_sp...  1.56 us

profile of v6, /device:TPU:1, one launch (start us, length us, event | category | flops | bytes accessed | tf_op | source)
XLA Modules:
  0.0 48.7 jit_solution(11919452743183326577)
XLA Ops:
  0.6 46.5 %tree_attention.1 = (bf16[128,4096]{1,0:T(8,128)(2,1)S(1)}, bf16[128,4096]{1,0:T(8,128)(2,1)S(1)}, f32[128,2,512]{2,1,0:T(2,128)S(1)}, f32[2,16,512]{2,1,0:T(8,128)S(1)}) custom-call(bf16[128,4096]{1,0:T(8,128)(2,1)} %bitcast.9, bf16[128,4096]{1,0:T(8,128)(2,1)} %bitcast.10, bf16[128,2,512]{2,1,0:T(2,128)(2,1)} %bitcast.11, bf16[2,16,512]{2,1,0:T(8,128)(2,1)} %bitcast.12, ...), custom_call_target="tpu_custom_call" | custom-call | tf_op jit(solution)/shard_map/tree_attention/pallas_call | solution.py:397
  47.1 1.6 %assemble.1 = (bf16[128,4096]{1,0:T(8,128)(2,1)}, bf16[128,4096]{1,0:T(8,128)(2,1)}, f32[128,2,512]{2,1,0:T(2,128)}, f32[2,16,512]{2,1,0:T(8,128)}) custom-call(bf16[128,4096]{1,0:T(8,128)(2,1)S(1)} %get-tuple-element.12.refs_0_, bf16[128,4096]{1,0:T(8,128)(2,1)S(1)} %get-tuple-element.13.refs_1_, f32[128,2,512]{2,1,0:T(2,128)S(1)} %get-tuple-element.14.refs_2_, ...), custom_call_target="tpu_custom_call" | custom-call | tf_op jit(solution)/shard_map/assemble/pallas_call | solution.py:469
